TPU v7x, 512 devices: a whole 4x8x8 slice. The times are simulated.
512 devices in a mesh: dom: 8 (over z), row: 8 (over x, y_lo), col: 8 (over y_hi, core).
Axes of the slice: x: 4, y: 8 (y_hi: 4, y_lo: 2; y = y_hi * 2 + y_lo), z: 8, core: 2. Of those that a mesh axis runs over, the one named last changes fastest.
Arguments:
- currents: bfloat16 [8, 64, 32768], P('dom', None, ('col', 'row')), may hold values from -6 to 6
- shared_basis: bfloat16 [8, 64, 32768], P('dom', None, 'col'), may hold values from -0.25 to 0.25
- self_v: bfloat16 [8, 16, 64, 64, 512], P('dom', 'row', 'col'), may hold values from -0.25 to 0.25
- self_u: bfloat16 [8, 16, 64, 64, 512], P('dom', 'row', 'col'), may hold values from -0.09375 to 0.09375
- self_rank: int32 [8, 16, 64], P('dom', 'row', 'col'), may hold values from 16 to 64
- coupling_u: bfloat16 [8, 16, 8, 16, 64, 512], P('dom', 'row', None, 'col'), may hold values from -0.0625 to 0.0625
- coupling_rank: int32 [8, 16, 8, 16], P('dom', 'row', None, 'col'), may hold values from 16 to 64
- link_tiles: int32 [8, 16, 8, 16], P('dom', 'row', None, 'col'), may hold values from 0 to 7
- incident: float32 [8, 64, 8192], P('dom', 'col', 'row'), may hold values from -6 to 6
Outputs:
- residual: float32 [8, 64, 8192], P('dom', 'col', 'row')
Inputs may be any that keep to these rules, and one draw needn't show every extreme that they name: `link_tiles`: entries may repeat within a list.
All inputs are finite; a program needn't handle non-finite values.
Results may differ from a plain program's by a relative error of at most 0.0022.
Values may be sent and summed in bfloat16 or wider, within the bound.
No kernel may reach another device: no remote copies, remote signals or barrier semaphores. Data moves between devices by JAX's collectives and lax.ppermute only.
A program may use at most 64 MiB of HBM per device.

v0:
```python
import jax
import jax.numpy as jnp
from jax import lax
from jax.sharding import PartitionSpec as P


def in_order(tiles, dim):
    tiles = jnp.moveaxis(tiles, 0, dim)
    dims = tiles.shape
    return tiles.reshape(*dims[:dim], dims[dim] * dims[dim + 1], *dims[dim + 2 :])


def from_everyone(value, axis):
    copies = jnp.broadcast_to(value, (lax.axis_size(axis), *value.shape))
    return lax.all_to_all(copies, axis, split_axis=0, concat_axis=0, tiled=True)


def collect(value, axis, dim):
    return in_order(from_everyone(value, axis), dim)


def cut_along(value, dim, length):
    before, after = (value.shape[:dim], value.shape[dim + 1 :])
    return jnp.moveaxis(value.reshape(*before, length, -1, *after), dim, 0)


def sent_and_summed(value, axis, dim):
    tiles = cut_along(value, dim, lax.axis_size(axis))
    arrived = lax.all_to_all(tiles, axis, split_axis=0, concat_axis=0, tiled=True)
    return arrived.sum(axis=0)


def shards(
    currents,
    shared_basis,
    self_v,
    self_u,
    self_rank,
    coupling_u,
    coupling_rank,
    link_tiles,
    incident,
):
    col_count = lax.axis_size("col")
    row_count = lax.axis_size("row")
    dom_count = lax.axis_size("dom")
    angles = currents.shape[1]
    tile_len = self_v.shape[-1]
    rank_len = self_v.shape[-2]
    own_tiles = currents.shape[2] // tile_len
    block_tiles = own_tiles * row_count
    window_rows = self_v.shape[1]
    link_count = link_tiles.shape[-1]
    gathered = collect(currents, "row", 2)
    current_tiles = gathered[0].reshape(angles, block_tiles, tile_len)
    levels = jnp.arange(rank_len, dtype=jnp.int32)
    keep_self = (levels[None, None, :] < self_rank[0][:, :, None]).astype(jnp.float32)
    selfproj = jnp.einsum(
        "tjkn,ajn->tjka", self_v[0], current_tiles, preferred_element_type=jnp.float32
    )
    selfproj = (selfproj * keep_self[..., None]).astype(jnp.bfloat16)
    bases = shared_basis[0].reshape(rank_len, block_tiles, tile_len)
    own_basis = lax.dynamic_slice_in_dim(bases, lax.axis_index("row") * own_tiles, own_tiles, 1)
    local_tiles = currents[0].reshape(angles, own_tiles, tile_len)
    projections = jnp.einsum(
        "kjn,ajn->jka", own_basis, local_tiles, preferred_element_type=jnp.float32
    ).astype(jnp.bfloat16)
    flat_proj = collect(projections, ("dom", "row"), 0)
    picks = jnp.arange(dom_count, dtype=jnp.int32)[None, :, None] * block_tiles + link_tiles[0]
    chosen = jnp.take(flat_proj, picks.reshape(-1), axis=0)
    chosen = chosen.reshape(window_rows, dom_count, link_count, rank_len, angles)
    keep_cpl = (levels < coupling_rank[0][..., None]).astype(jnp.bfloat16)
    chosen = chosen * keep_cpl[..., None]
    field_self = jnp.einsum(
        "tjkn,tjka->atn", self_u[0], selfproj, preferred_element_type=jnp.float32
    )
    field_cpl = jnp.einsum(
        "temkn,temka->atn", coupling_u[0], chosen, preferred_element_type=jnp.float32
    )
    summed = sent_and_summed(
        (field_self + field_cpl).reshape(
            angles // col_count * lax.axis_size("col"), window_rows * tile_len
        ),
        "col",
        0,
    )
    return (incident[0] - summed)[None]


def solution(mesh):
    return jax.shard_map(
        shards,
        mesh=mesh,
        in_specs=(
            P("dom", None, ("col", "row")),
            P("dom", None, "col"),
            P("dom", "row", "col", None, None),
            P("dom", "row", "col", None, None),
            P("dom", "row", "col"),
            P("dom", "row", None, "col", None, None),
            P("dom", "row", None, "col"),
            P("dom", "row", None, "col"),
            P("dom", "col", "row"),
        ),
        out_specs=P("dom", "col", "row"),
        check_vma=False,
    )
```

profile of v0, /device:TPU:1, one launch (start us, length us, event | category | flops | bytes accessed | tf_op | source)
XLA Modules:
  0.0 70.8 jit_solution(9673199422237855046)
XLA Ops:
  0.0 0.0 copy-start
  0.0 0.0 copy-start.1
  0.0 1.9 %broadcast_in_dim.22 = bf16[8,1,64,512]{3,2,1,0:T(8,128)(2,1)} broadcast(bf16[64,512]{1,0:T(8,128)(2,1)} %bitcast.71), dimensions={2,3} | broadcast | bytes 589824 | tf_op jit(solution)/shard_map/broadcast_in_dim | solution.py:14
  1.9 5.9 %all-to-all-start = ((bf16[8,1,64,512]{3,2,1,0:T(8,128)(2,1)}), bf16[8,1,64,512]{3,2,1,0:T(8,128)(2,1)}, u32[]{:S(2)}, u32[]{:S(2)}) async-start(bf16[8,1,64,512]{3,2,1,0:T(8,128)(2,1)} %broadcast_in_dim.22), calls=%async_computation | async-start | bytes 1048576 | tf_op jit(solution)/shard_map/all_to_all | solution.py:15
  7.7 1.2 %copy.38 = bf16[8,8,8,512]{3,2,1,0:T(8,128)(2,1)S(1)} copy(bf16[8,8,8,512]{3,1,2,0:T(8,128)(2,1)} %bitcast.70) | data formatting | bytes 1048576
  8.9 0.0 copy-start.3
  8.9 0.0 copy-start.4
  8.9 0.0 copy-start.5
  9.0 0.1 constant_dynamic-slice_fusion
  9.1 0.0 copy-done.1
  9.1 0.1 convolution_convert_fusion
  9.3 0.2 broadcast_in_dim.24
  9.5 1.5 %reshape.83 = bf16[64,2,2048]{2,1,0:T(2,128)(2,1)} reshape(bf16[64,1,64,64]{3,2,1,0:T(8,128)(2,1)S(1)} %broadcast_in_dim.24) | data formatting | bytes 1048576
  11.1 4.3 %all-to-all-done = bf16[8,1,64,512]{3,2,1,0:T(8,128)(2,1)} async-done(((bf16[8,1,64,512]{3,2,1,0:T(8,128)(2,1)}), bf16[8,1,64,512]{3,2,1,0:T(8,128)(2,1)}, u32[]{:S(2)}, u32[]{:S(2)}) %all-to-all-start) | async-done | bytes 524320 | tf_op jit(solution)/shard_map/all_to_all | solution.py:15
  15.3 13.7 %all-to-all-start.1 = ((bf16[64,2,2048]{2,1,0:T(2,128)(2,1)}), bf16[64,2,2048]{2,1,0:T(2,128)(2,1)}, u32[]{:S(2)}, u32[]{:S(2)}) async-start(bf16[64,2,2048]{2,1,0:T(2,128)(2,1)} %reshape.83), calls=%async_computation.1 | async-start | bytes 1048576 | tf_op jit(solution)/shard_map/all_to_all | solution.py:15
  29.1 0.0 copy-done.3
  29.1 0.1 copy.30
  29.2 0.1 add.56.clone
  29.3 0.1 add.61
  29.4 0.1 squeeze.18
  29.5 0.1 copy.28
  29.6 0.0 copy-done.4
  29.6 0.1 copy.32
  29.7 0.0 copy-done.5
  29.7 0.1 fusion.28
  29.8 0.1 compare_convert_fusion
  29.9 2.6 %fusion.8 = f32[2,64,512]{2,1,0:T(8,128)S(1)} fusion(bf16[1,2,8,64,512]{4,3,2,1,0:T(8,128)(2,1)} %param.12, bf16[1,2,8,64,512]{4,3,2,1,0:T(8,128)(2,1)} %param.11, bf16[8,1,64,512]{3,2,1,0:T(8,128)(2,1)} %all-to-all-done, f32[2,8,64]{2,1,0:T(8,128)S(1)} %fusion.28), kind=kOutput, calls=%fused_computation.8 | convolution fusion | flops 134348800 | bytes 2887680 | tf_op jit(solution)/shard_map/tjkn,tjka->atn/dot_general | solution.py:74
  32.5 12.4 %all-to-all-done.1 = bf16[64,2,2048]{2,1,0:T(2,128)(2,1)} async-done(((bf16[64,2,2048]{2,1,0:T(2,128)(2,1)}), bf16[64,2,2048]{2,1,0:T(2,128)(2,1)}, u32[]{:S(2)}, u32[]{:S(2)}) %all-to-all-start.1) | async-done | bytes 524320 | tf_op jit(solution)/shard_map/all_to_all | solution.py:15
  44.9 2.3 %reshape.84 = bf16[64,1,64,64]{3,2,1,0:T(8,128)(2,1)S(1)} reshape(bf16[64,2,2048]{2,1,0:T(2,128)(2,1)} %all-to-all-done.1) | data formatting | bytes 1048576
  47.2 1.4 %gather_fusion = bf16[32,64,64]{2,1,0:T(8,128)(2,1)} fusion(bf16[64,64,64]{2,1,0:T(8,128)(2,1)S(1)} %bitcast.67, s32[1024]{0:T(1024)S(1)} %pad_clamp_fusion), kind=kCustom, calls=%fused_computation | custom fusion | bytes 524416 | tf_op jit(solution)/shard_map/jit(_take)/gather | solution.py:70
  48.6 1.3 %copy.31 = bf16[2,8,2,64,64]{3,4,2,0,1:T(8,128)(2,1)S(1)} copy(bf16[2,8,2,64,64]{4,3,2,1,0:T(8,128)(2,1)} %bitcast.68) | data formatting | bytes 524288 | tf_op jit(solution)/shard_map/jit(_take)/gather | solution.py:70
  49.9 0.0 copy-done
  49.9 0.0 copy-start.2
  49.9 0.6 fusion.12
  50.5 0.2 copy.34
  50.7 0.2 reshape_reshape.3
  51.0 19.2 %all_to_all.15 = f32[8,8,1024]{2,1,0:T(8,128)S(1)} all-to-all(f32[8,8,1024]{2,1,0:T(8,128)S(1)} %reshape_reshape.3), channel_id=1, replica_groups=mesh['dom'=8,'row'=8,'col'=8] {'col'}, dimensions={0} | all-to-all | bytes 524288 | tf_op jit(solution)/shard_map/all_to_all | solution.py:29
  70.2 0.0 copy-done.2
  70.2 0.6 bitcast_subtract_fusion
  (5 shorter events, 0.0 us)
Async XLA Ops:
  0.0 49.9 %copy-start = (bf16[1,2,8,2,64,512]{5,4,3,2,1,0:T(8,128)(2,1)S(1)}, bf16[1,2,8,2,64,512]{5,4,3,2,1,0:T(8,128)(2,1)}, u32[]{:S(2)}) copy-start(bf16[1,2,8,2,64,512]{5,4,3,2,1,0:T(8,128)(2,1)} %param.14) | copy-start | bytes 6291460
  0.0 9.1 %copy-start.1 = (bf16[1,64,512]{2,1,0:T(8,128)(2,1)S(1)}, bf16[1,64,512]{2,1,0:T(8,128)(2,1)}, u32[]{:S(2)}) copy-start(bf16[1,64,512]{2,1,0:T(8,128)(2,1)} %param.9) | copy-start | bytes 196612
  1.9 13.5 %all-to-all-start = ((bf16[8,1,64,512]{3,2,1,0:T(8,128)(2,1)}), bf16[8,1,64,512]{3,2,1,0:T(8,128)(2,1)}, u32[]{:S(2)}, u32[]{:S(2)}) async-start(bf16[8,1,64,512]{3,2,1,0:T(8,128)(2,1)} %broadcast_in_dim.22), calls=%async_computation | async-start | bytes 1048576 | tf_op jit(solution)/shard_map/all_to_all | solution.py:15
  8.9 20.2 %copy-start.3 = (s32[1,2,8,2]{2,3,1,0:T(2,128)S(1)}, s32[1,2,8,2]{2,3,1,0:T(2,128)}, u32[]{:S(2)}) copy-start(s32[1,2,8,2]{2,3,1,0:T(2,128)} %param.16) | copy-start | bytes 388
  8.9 20.6 %copy-start.4 = (s32[1,2,8,2]{2,3,1,0:T(2,128)S(1)}, s32[1,2,8,2]{2,3,1,0:T(2,128)}, u32[]{:S(2)}) copy-start(s32[1,2,8,2]{2,3,1,0:T(2,128)} %param.15) | copy-start | bytes 388
  8.9 20.7 %copy-start.5 = (s32[1,2,8]{2,1,0:T(2,128)S(1)}, s32[1,2,8]{2,1,0:T(2,128)}, u32[]{:S(2)}) copy-start(s32[1,2,8]{2,1,0:T(2,128)} %param.13) | copy-start | bytes 196
  15.3 29.5 %all-to-all-start.1 = ((bf16[64,2,2048]{2,1,0:T(2,128)(2,1)}), bf16[64,2,2048]{2,1,0:T(2,128)(2,1)}, u32[]{:S(2)}, u32[]{:S(2)}) async-start(bf16[64,2,2048]{2,1,0:T(2,128)(2,1)} %reshape.83), calls=%async_computation.1 | async-start | bytes 1048576 | tf_op jit(solution)/shard_map/all_to_all | solution.py:15
  49.9 20.3 %copy-start.2 = (f32[1,8,1024]{2,1,0:T(8,128)S(1)}, f32[1,8,1024]{2,1,0:T(8,128)}, u32[]{:S(2)}) copy-start(f32[1,8,1024]{2,1,0:T(8,128)} %param.17) | copy-start | bytes 98308
where the time goes:
time: 71.3 us; the launch traced here: 70.8 us
  starting transfers between devices  19.6 us (27%)
  blocking collectives  19.2 us (27%)
  waiting for transfers between devices  16.7 us (23%)
  local copies, waits for them, and re-layouts  11 us (15%)
  matrix products  3.35 us (5%)
  other arithmetic  0.82 us (1%)
    all_to_all x2, starting transfers between devices, from_everyone(): return lax.all_to_all(copies, axis, split_axis=0, concat_axis=0, tiled=True)  19.6 us
    all_to_all x1, blocking collectives, sent_and_summed(): lax.all_to_all(tiles, axis, split_axis=0, concat_axis=0, tiled=True)  19.2 us
    all_to_all x2, waiting for transfers between devices, from_everyone(): return lax.all_to_all(copies, axis, split_axis=0, concat_axis=0, tiled=True)  16.7 us
    unnamed x16, local copies, waits for them, and re-layouts  5.17 us
    gather x2, local copies, waits for them, and re-layouts, shards(): chosen = jnp.take(flat_proj, picks.reshape(-1), axis=0)  2.71 us
    dot_general x1, matrix products, shards(): jnp.einsum('tjkn,tjka->atn', self_u[0], selfproj, preferred_element_type=...  2.6 us
    broadcast_in_dim x2, local copies, waits for them, and re-layouts, from_everyone(): copies = jnp.broadcast_to(value, (lax.axis_size(axis), *value.shape))  2.1 us
  transfers between devices with their start and end apart: 2, of which 2 were waited for; matrix products, arithmetic and copies ran while one was open for 9% of the time, Pallas kernels for 0%

commit v1 on v0

v1 whole, which is shorter than its diff:
```python
import jax
import jax.numpy as jnp
from jax import lax
from jax.experimental import pallas as pl
from jax.experimental.pallas import tpu as pltpu
from jax.sharding import PartitionSpec as P

BF = jnp.bfloat16
F32 = jnp.float32
NT = (((1,), (1,)), ((), ()))


def exchange(value, axis):
    return lax.all_to_all(value, axis, split_axis=0, concat_axis=0, tiled=True)


def low_lanes(shape):
    return lax.broadcasted_iota(jnp.int32, shape, 1) < shape[1] // 2


def project_kernel(where, currents, basis, out):
    proj = lax.dot_general(currents[...], basis[...], NT, preferred_element_type=F32)
    half = proj.shape[0] // 2
    packed = jnp.concatenate([proj[:half], proj[half:]], axis=1).astype(BF)
    for peer in range(out.shape[0]):
        out[peer] = packed


def pack_kernel(arrived, currents, out):
    tile = currents.shape[1]
    half, lanes = arrived.shape[1:]
    low = low_lanes((half, lanes))
    rows = []
    for pair in range(arrived.shape[0] // 2):
        even = arrived[2 * pair].astype(F32)
        odd = arrived[2 * pair + 1].astype(F32)
        top = jnp.where(low, even, pltpu.roll(odd, lanes // 2, 1))
        bottom = jnp.where(low, pltpu.roll(even, lanes // 2, 1), odd)
        rows.append(jnp.concatenate([top, bottom], axis=0).astype(BF))
    own = currents[...]
    for peer in range(out.shape[0]):
        out[peer, :, :tile] = own
        for pair, value in enumerate(rows):
            out[peer, :, tile + pair * lanes : tile + (pair + 1) * lanes] = value


def field_kernel(self_rank, cpl_rank, links, arrived, v, u, cu, out, left, picked):
    rows, tiles, ranks, tile = v.shape
    parts, link_count = cu.shape[1:3]
    angles = arrived.shape[1]
    lanes = 2 * ranks
    low = low_lanes((angles, lanes))
    level = lax.broadcasted_iota(jnp.int32, (angles, lanes), 1)
    level = jnp.where(low, level, level - ranks)
    for pair in range(tiles // 2):
        first, second = 2 * pair, 2 * pair + 1
        both = jnp.concatenate([arrived[first, :, :tile], arrived[second, :, :tile]], axis=0)
        for t in range(rows):
            factors = v[t, first : second + 1].reshape(lanes, tile)
            product = lax.dot_general(both, factors, NT, preferred_element_type=F32)
            value = jnp.where(low, product[:angles], product[angles:])
            limit = jnp.where(low, self_rank[t, first], self_rank[t, second])
            value = jnp.where(level < limit, value, 0.0)
            left[t, :, pair * lanes : (pair + 1) * lanes] = value.astype(BF)
    for t in range(rows):
        for e in range(parts):
            at = tile + (e // 2) * lanes
            one = arrived[links[t, e, 0], :, at : at + lanes].astype(F32)
            two = arrived[links[t, e, 1], :, at : at + lanes].astype(F32)
            if e % 2 == 0:
                two = pltpu.roll(two, ranks, 1)
            else:
                one = pltpu.roll(one, ranks, 1)
            value = jnp.where(low, one, two)
            limit = jnp.where(low, cpl_rank[t, e, 0], cpl_rank[t, e, 1])
            value = jnp.where(level < limit, value, 0.0)
            picked[t, :, e * lanes : (e + 1) * lanes] = value.astype(BF)
    for t in range(rows):
        field = jnp.dot(left[t], u[t].reshape(tiles * ranks, tile), preferred_element_type=F32)
        field += jnp.dot(
            picked[t], cu[t].reshape(parts * link_count * ranks, tile), preferred_element_type=F32
        )
        out[:, t * tile : (t + 1) * tile] = field.astype(out.dtype)


def shards(
    currents, shared_basis, self_v, self_u, self_rank, coupling_u, coupling_rank, link_tiles, incident
):
    row_count = lax.axis_size("row")
    dom_count = lax.axis_size("dom")
    col_count = lax.axis_size("col")
    _, angles, tile = currents.shape
    _, window_rows, tiles, ranks, _ = self_v.shape
    link_count = link_tiles.shape[-1]
    vmem = pl.BlockSpec(memory_space=pltpu.VMEM)
    smem = pl.BlockSpec(memory_space=pltpu.SMEM)
    own = currents[0]
    where = lax.axis_index("row").astype(jnp.int32).reshape(1)
    outgoing = pl.pallas_call(
        project_kernel,
        out_shape=jax.ShapeDtypeStruct((dom_count, angles // 2, 2 * ranks), BF),
        grid_spec=pltpu.PrefetchScalarGridSpec(
            num_scalar_prefetch=1,
            grid=(1,),
            in_specs=[
                pl.BlockSpec((angles, tile), lambda i, w: (0, 0)),
                pl.BlockSpec((ranks, tile), lambda i, w: (0, w[0])),
            ],
            out_specs=pl.BlockSpec((dom_count, angles // 2, 2 * ranks), lambda i, w: (0, 0, 0)),
        ),
        name="project",
    )(where, own, shared_basis[0])
    arrived = exchange(outgoing, "dom")
    outgoing = pl.pallas_call(
        pack_kernel,
        out_shape=jax.ShapeDtypeStruct((row_count, angles, tile + dom_count * ranks), BF),
        in_specs=[vmem, vmem],
        out_specs=vmem,
        name="pack",
    )(arrived, own)
    arrived = exchange(outgoing, "row")
    partial = pl.pallas_call(
        field_kernel,
        out_shape=jax.ShapeDtypeStruct((angles, window_rows * tile), BF),
        in_specs=[smem, smem, smem, vmem, vmem, vmem, vmem],
        out_specs=vmem,
        scratch_shapes=[
            pltpu.VMEM((window_rows, angles, tiles * ranks), BF),
            pltpu.VMEM((window_rows, angles, dom_count * link_count * ranks), BF),
        ],
        name="field",
    )(self_rank[0], coupling_rank[0], link_tiles[0], arrived, self_v[0], self_u[0], coupling_u[0])
    arrived = exchange(partial.reshape(col_count, angles // col_count, window_rows * tile), "col")
    return (incident[0] - arrived.astype(F32).sum(axis=0))[None]


def solution(mesh):
    return jax.shard_map(
        shards,
        mesh=mesh,
        in_specs=(
            P("dom", None, ("col", "row")),
            P("dom", None, "col"),
            P("dom", "row", "col", None, None),
            P("dom", "row", "col", None, None),
            P("dom", "row", "col"),
            P("dom", "row", None, "col", None, None),
            P("dom", "row", None, "col"),
            P("dom", "row", None, "col"),
            P("dom", "col", "row"),
        ),
        out_specs=P("dom", "col", "row"),
        check_vma=False,
    )
```

time: 71.3 us -> 64.2 us (0.900)
  blocking collectives: 19.2 us -> 35.7 us
  starting transfers between devices: 19.6 us -> 5.03 us
  local copies, waits for them, and re-layouts: 11 us -> 2.34 us
  Pallas kernels: 0 us -> 7.93 us
  waiting for transfers between devices: 16.7 us -> 12.1 us
  matrix products: 3.35 us -> 0 us
    all_to_all x1 -> x2, blocking collectives: 19.2 us -> 35.7 us  [exchange(): return lax.all_to_all(value, axis, split_axis=0, concat_axis=0, tiled=True)]
    all_to_all x2 -> x1, starting transfers between devices: 19.6 us -> 5.03 us  [exchange(): return lax.all_to_all(value, axis, split_axis=0, concat_axis=0, tiled=True)]
    pallas_call x0 -> x3, Pallas kernels: none -> 7.93 us  [the longest x1 4.16 us: shards(): pl.pallas_call(field_kernel, out_shape=jax.ShapeDtypeStruct((angles, wind...]
    all_to_all x2 -> x1, waiting for transfers between devices: 16.7 us -> 12.1 us  [exchange(): return lax.all_to_all(value, axis, split_axis=0, concat_axis=0, tiled=True)]
    unnamed x16 -> x8, local copies, waits for them, and re-layouts: 5.17 us -> 0.98 us
    dot_general x3 -> x0, matrix products: 3.35 us -> none  [the longest x1 2.6 us: shards(): jnp.einsum('tjkn,tjka->atn', self_u[0], selfproj, preferred_element_type=...]
    gather x2 -> x0, local copies, waits for them, and re-layouts: 2.71 us -> none  [shards(): chosen = jnp.take(flat_proj, picks.reshape(-1), axis=0)]
    broadcast_in_dim x2 -> x0, local copies, waits for them, and re-layouts: 2.1 us -> none  [from_everyone(): copies = jnp.broadcast_to(value, (lax.axis_size(axis), *value.shape))]
  transfers between devices with their start and end apart: 2 -> 1, of which waited for: 2 -> 1; matrix products, arithmetic and copies ran while one was open for 9% -> 2% of each run, Pallas kernels for 0% -> 0%
where the time goes in v1:
time: 64.2 us; the launch traced here: 63.8 us
  blocking collectives  35.7 us (56%)
  waiting for transfers between devices  12.1 us (19%)
  Pallas kernels  7.93 us (12%)
  starting transfers between devices  5.03 us (8%)
  local copies, waits for them, and re-layouts  2.34 us (4%)
    all_to_all x2, blocking collectives, exchange(): return lax.all_to_all(value, axis, split_axis=0, concat_axis=0, tiled=True)  35.7 us
    all_to_all x1, waiting for transfers between devices, exchange(): return lax.all_to_all(value, axis, split_axis=0, concat_axis=0, tiled=True)  12.1 us
    all_to_all x1, starting transfers between devices, exchange(): return lax.all_to_all(value, axis, split_axis=0, concat_axis=0, tiled=True)  5.03 us
    pallas_call x1, Pallas kernels, shards(): pl.pallas_call(field_kernel, out_shape=jax.ShapeDtypeStruct((angles, wind...  4.16 us
    pallas_call x1, Pallas kernels, shards(): pl.pallas_call(pack_kernel, out_shape=jax.ShapeDtypeStruct((row_count, an...  2.04 us
    pallas_call x1, Pallas kernels, shards(): pl.pallas_call(project_kernel, out_shape=jax.ShapeDtypeStruct((dom_count,...  1.73 us
  transfers between devices with their start and end apart: 1, of which 1 were waited for; matrix products, arithmetic and copies ran while one was open for 2% of the time, Pallas kernels for 0%

profile of v1, /device:TPU:1, one launch (start us, length us, event | category | flops | bytes accessed | tf_op | source)
XLA Modules:
  0.0 63.8 jit_solution(10800691709248781154)
XLA Ops:
  0.0 0.0 copy-start.2
  0.0 0.0 copy-start.3
  0.0 1.7 %project.1 = bf16[8,32,128]{2,1,0:T(8,128)(2,1)} custom-call(s32[1]{0:T(128)} %bitcast.3.where, bf16[64,512]{1,0:T(8,128)(2,1)} %bitcast.17, bf16[64,4096]{1,0:T(8,128)(2,1)} %bitcast.16), custom_call_target="tpu_custom_call" | custom-call | tf_op jit(solution)/shard_map/project/pallas_call | solution.py:99
  1.7 18.2 %all_to_all.15.arrived = bf16[8,32,128]{2,1,0:T(8,128)(2,1)} all-to-all(bf16[8,32,128]{2,1,0:T(8,128)(2,1)} %project.1), channel_id=1, replica_groups=mesh['dom'=8,'row'=8,'col'=8] {'dom'}, dimensions={0} | all-to-all | bytes 131072 | tf_op jit(solution)/shard_map/all_to_all | solution.py:14
  19.9 2.0 %pack.1 = bf16[8,64,1024]{2,1,0:T(8,128)(2,1)} custom-call(bf16[8,32,128]{2,1,0:T(8,128)(2,1)} %all_to_all.15.arrived, bf16[64,512]{1,0:T(8,128)(2,1)} %bitcast.18), custom_call_target="tpu_custom_call" | custom-call | tf_op jit(solution)/shard_map/pack/pallas_call | solution.py:114
  22.0 5.0 %all-to-all-start.1 = ((bf16[8,64,1024]{2,1,0:T(8,128)(2,1)}), bf16[8,64,1024]{2,1,0:T(8,128)(2,1)S(1)}, u32[]{:S(2)}, u32[]{:S(2)}) async-start(bf16[8,64,1024]{2,1,0:T(8,128)(2,1)} %pack.1), calls=%async_computation.1 | async-start | bytes 2097152 | tf_op jit(solution)/shard_map/all_to_all | solution.py:14
  27.0 0.0 copy-done.2
  27.0 0.7 %copy.10.cpl_rank = s32[2,8,2]{2,1,0:T(8,128)} copy(s32[2,8,2]{1,2,0:T(2,128)S(1)} %bitcast.19) | data formatting | bytes 256 | tf_op jit(solution)/shard_map/squeeze | solution.py:132
  27.7 0.0 copy-done.3
  27.7 0.7 %copy.11.links = s32[2,8,2]{2,1,0:T(8,128)} copy(s32[2,8,2]{1,2,0:T(2,128)S(1)} %bitcast.20) | data formatting | bytes 256 | tf_op jit(solution)/shard_map/squeeze | solution.py:132
  28.4 12.1 %all-to-all-done.1.arrived = bf16[8,64,1024]{2,1,0:T(8,128)(2,1)S(1)} async-done(((bf16[8,64,1024]{2,1,0:T(8,128)(2,1)}), bf16[8,64,1024]{2,1,0:T(8,128)(2,1)S(1)}, u32[]{:S(2)}, u32[]{:S(2)}) %all-to-all-start.1) | async-done | bytes 1048608 | tf_op jit(solution)/shard_map/all_to_all | solution.py:14
  40.5 0.0 copy-start
  40.5 1.0 %copy-done = bf16[8,64,1024]{2,1,0:T(8,128)(2,1)} copy-done((bf16[8,64,1024]{2,1,0:T(8,128)(2,1)}, bf16[8,64,1024]{2,1,0:T(8,128)(2,1)S(1)}, u32[]{:S(2)}) %copy-start) | copy-done | bytes 1048600
  41.5 0.0 copy-start.1
  41.5 4.2 %field.1 = bf16[64,1024]{1,0:T(8,128)(2,1)} custom-call(s32[2,8]{1,0:T(2,128)} %bitcast.21, s32[2,8,2]{2,1,0:T(8,128)} %copy.10.cpl_rank, s32[2,8,2]{2,1,0:T(8,128)} %copy.11.links, bf16[8,64,1024]{2,1,0:T(8,128)(2,1)} %copy-done, bf16[2,8,64,512]{3,2,1,0:T(8,128)(2,1)} %bitcast.13, bf16[2,8,64,512]{3,2,1,0:T(8,128)(2,1)} %bitcast.14, ...), custom_call_target="tpu_custom_call" | custom-call | tf_op jit(solution)/shard_map/field/pallas_call | solution.py:122
  45.6 17.5 %all_to_all.16 = bf16[8,8,1024]{2,1,0:T(8,128)(2,1)S(1)} all-to-all(bf16[8,8,1024]{2,1,0:T(8,128)(2,1)} %bitcast.15), channel_id=1, replica_groups=mesh['dom'=8,'row'=8,'col'=8] {'col'}, dimensions={0} | all-to-all | bytes 262144 | tf_op jit(solution)/shard_map/all_to_all | solution.py:14
  63.2 0.0 copy-done.1
  63.2 0.6 bitcast_subtract_fusion
  (1 shorter events, 0.0 us)
Async XLA Ops:
  0.0 27.0 %copy-start.2 = (s32[1,2,8,2]{2,3,1,0:T(2,128)S(1)}, s32[1,2,8,2]{2,3,1,0:T(2,128)}, u32[]{:S(2)}) copy-start(s32[1,2,8,2]{2,3,1,0:T(2,128)} %param.15) | copy-start | bytes 388
  0.0 27.7 %copy-start.3 = (s32[1,2,8,2]{2,3,1,0:T(2,128)S(1)}, s32[1,2,8,2]{2,3,1,0:T(2,128)}, u32[]{:S(2)}) copy-start(s32[1,2,8,2]{2,3,1,0:T(2,128)} %param.16) | copy-start | bytes 388
  22.0 18.5 %all-to-all-start.1 = ((bf16[8,64,1024]{2,1,0:T(8,128)(2,1)}), bf16[8,64,1024]{2,1,0:T(8,128)(2,1)S(1)}, u32[]{:S(2)}, u32[]{:S(2)}) async-start(bf16[8,64,1024]{2,1,0:T(8,128)(2,1)} %pack.1), calls=%async_computation.1 | async-start | bytes 2097152 | tf_op jit(solution)/shard_map/all_to_all | solution.py:14
  40.5 1.0 %copy-start = (bf16[8,64,1024]{2,1,0:T(8,128)(2,1)}, bf16[8,64,1024]{2,1,0:T(8,128)(2,1)S(1)}, u32[]{:S(2)}) copy-start(bf16[8,64,1024]{2,1,0:T(8,128)(2,1)S(1)} %all-to-all-done.1.arrived) | copy-start | bytes 3145732
  41.5 21.7 %copy-start.1 = (f32[1,8,1024]{2,1,0:T(8,128)S(1)}, f32[1,8,1024]{2,1,0:T(8,128)}, u32[]{:S(2)}) copy-start(f32[1,8,1024]{2,1,0:T(8,128)} %param.17) | copy-start | bytes 98308

commit v2 on v1

v2 whole, which is shorter than its diff:
```python
import jax
import jax.numpy as jnp
from jax import lax
from jax.experimental import pallas as pl
from jax.experimental.pallas import tpu as pltpu
from jax.sharding import PartitionSpec as P


BF = jnp.bfloat16
F32 = jnp.float32
NT = (((1,), (1,)), ((), ()))
ONCHIP = pl.BlockSpec(memory_space=pltpu.VMEM)
SCALARS = pl.BlockSpec(memory_space=pltpu.SMEM)
ANYWHERE = pl.BlockSpec(memory_space=pl.ANY)
LIMIT = pltpu.CompilerParams(vmem_limit_bytes=16 * 2**20)


def exchange(value, axis):
    return lax.all_to_all(value, axis, split_axis=0, concat_axis=0, tiled=True)


def swap(value, axis, bits):
    return lax.ppermute(value, axis, [(i, i ^ bits) for i in range(lax.axis_size(axis))])


def onchip(value):
    return pltpu.with_memory_space_constraint(value, pltpu.VMEM)


def inhbm(value):
    return pltpu.with_memory_space_constraint(value, pltpu.HBM)


def low_lanes(shape):
    return lax.broadcasted_iota(jnp.int32, shape, 1) < shape[1] // 2


def project_kernel(currents, basis, out, own, own_basis, arrivals):
    tile = currents.shape[1]
    at = pl.multiple_of(lax.axis_index("row") * tile, tile)
    copies = [
        pltpu.make_async_copy(basis.at[:, pl.ds(at, tile)], own_basis, arrivals.at[0]),
        pltpu.make_async_copy(currents, own, arrivals.at[1]),
    ]
    for copy in copies:
        copy.start()
    for copy in copies:
        copy.wait()
    proj = lax.dot_general(own[...], own_basis[...], NT, preferred_element_type=F32)
    half = proj.shape[0] // 2
    packed = jnp.concatenate([proj[:half], proj[half:]], axis=1).astype(BF)
    for peer in range(out.shape[0]):
        out[peer] = packed


def limits_kernel(self_rank, cpl_rank, out):
    rows, pairs = self_rank.shape[0], self_rank.shape[1] // 2
    low = low_lanes((1, out.shape[-1]))
    for t in range(rows):
        for q in range(pairs):
            out[t, q : q + 1] = jnp.where(low, self_rank[t, 2 * q], self_rank[t, 2 * q + 1])
        for e in range(cpl_rank.shape[1]):
            at = pairs + e
            out[t, at : at + 1] = jnp.where(low, cpl_rank[t, e, 0], cpl_rank[t, e, 1])


def pair_of(slot):
    return slot ^ (lax.axis_index("row") // 2)


def projected(currents, factors, limits):
    odd = lax.axis_index("row") % 2
    angles = currents.shape[1]
    lanes = limits.shape[-1]
    both = jnp.concatenate([currents[odd], currents[1 - odd]], axis=0)
    product = lax.dot_general(
        both, factors.reshape(lanes, factors.shape[-1]), NT, preferred_element_type=F32
    )
    value = jnp.where(low_lanes((angles, lanes)), product[:angles], product[angles:])
    return jnp.where(levels((angles, lanes)) < limits, value, 0.0).astype(BF)


def levels(shape):
    level = lax.broadcasted_iota(jnp.int32, shape, 1)
    return jnp.where(low_lanes(shape), level, level - shape[1] // 2)


def self_kernel(limits, near, far2, far6, v_hbm, u_hbm, out, v, u, arrivals):
    rows, _, ranks, tile = v.shape
    fetch = [
        pltpu.make_async_copy(src, dst, arrivals.at[i])
        for i, (src, dst) in enumerate(((v_hbm, v), (u_hbm, u)))
    ]
    for copy in fetch:
        copy.start()
    fetch[0].wait()
    slots = ((0, near), (1, far2), (3, far6))
    left = []
    for t in range(rows):
        for slot, currents in slots:
            pair = pair_of(slot)
            left.append(
                projected(currents, v[t, pl.ds(2 * pair, 2)], limits[t, pl.ds(pair, 1)])
            )
    fetch[1].wait()
    for t in range(rows):
        total = None
        for i, (slot, _) in enumerate(slots):
            factors = u[t, pl.ds(2 * pair_of(slot), 2)].reshape(2 * ranks, tile)
            part = jnp.dot(left[t * len(slots) + i], factors, preferred_element_type=F32)
            total = part if total is None else total + part
        out[:, t * tile : (t + 1) * tile] = total


def coupled_kernel(
    links, limits, arrived, far4, field, cu, v_hbm, u_hbm, out, picked, last_v, last_u, arrivals
):
    rows, parts, link_count, ranks, tile = cu.shape
    angles = field.shape[0]
    half, lanes = arrived.shape[1:]
    block_tiles = arrived.shape[0] // parts
    pairs = limits.shape[1] - parts
    low = low_lanes((half, lanes))
    level = levels((angles, lanes))
    last = pl.ds(2 * pair_of(2), 2)
    fetch = [
        pltpu.make_async_copy(src.at[:, last], dst, arrivals.at[i])
        for i, (src, dst) in enumerate(((v_hbm, last_v), (u_hbm, last_u)))
    ]
    for copy in fetch:
        copy.start()
    for t in range(rows):
        for e in range(parts):
            one = arrived[e * block_tiles + links[t, e, 0]].astype(F32)
            two = arrived[e * block_tiles + links[t, e, 1]].astype(F32)
            top = jnp.where(low, one, pltpu.roll(two, ranks, 1))
            bottom = jnp.where(low, pltpu.roll(one, ranks, 1), two)
            value = jnp.concatenate([top, bottom], axis=0)
            value = jnp.where(level < limits[t, pairs + e : pairs + e + 1], value, 0.0)
            picked[t, :, e * lanes : (e + 1) * lanes] = value.astype(BF)
    totals = []
    for t in range(rows):
        total = field[:, t * tile : (t + 1) * tile]
        total += jnp.dot(
            picked[t], cu[t].reshape(parts * link_count * ranks, tile), preferred_element_type=F32
        )
        totals.append(total)
    for copy in fetch:
        copy.wait()
    for t in range(rows):
        left = projected(far4, last_v[t], limits[t, pl.ds(pair_of(2), 1)])
        total = totals[t] + jnp.dot(
            left, last_u[t].reshape(lanes, tile), preferred_element_type=F32
        )
        out[:, t * tile : (t + 1) * tile] = total.astype(out.dtype)


def residual(
    currents, shared_basis, self_v, self_u, self_rank, coupling_u, coupling_rank, link_tiles, incident
):
    row_count = lax.axis_size("row")
    dom_count = lax.axis_size("dom")
    col_count = lax.axis_size("col")
    _, angles, tile = currents.shape
    _, window_rows, tiles, ranks, _ = self_v.shape
    link_count = link_tiles.shape[-1]
    own = currents[0]
    neighbour = swap(own, "row", 1)
    outgoing = pl.pallas_call(
        project_kernel,
        out_shape=pltpu.VMEM((dom_count * row_count, angles // 2, 2 * ranks), BF),
        in_specs=[ANYWHERE, ANYWHERE],
        out_specs=ONCHIP,
        scratch_shapes=[
            pltpu.VMEM((angles, tile), BF),
            pltpu.VMEM((ranks, tile), BF),
            pltpu.SemaphoreType.DMA((2,)),
        ],
        compiler_params=LIMIT,
        name="project",
    )(inhbm(own), inhbm(shared_basis[0]))
    arrived = exchange(outgoing, ("dom", "row"))
    near = jnp.stack([own, neighbour])
    far = {}
    for bits in (2, 6, 4):
        far[bits] = swap(near, "row", bits)
    limits = pl.pallas_call(
        limits_kernel,
        out_shape=pltpu.VMEM((window_rows, tiles // 2 + dom_count, 2 * ranks), jnp.int32),
        in_specs=[SCALARS, SCALARS],
        out_specs=ONCHIP,
        compiler_params=LIMIT,
        name="limits",
    )(self_rank[0], coupling_rank[0])
    field = pl.pallas_call(
        self_kernel,
        out_shape=pltpu.VMEM((angles, window_rows * tile), F32),
        in_specs=[ONCHIP] * 4 + [ANYWHERE] * 2,
        out_specs=ONCHIP,
        scratch_shapes=[
            pltpu.VMEM(self_v.shape[1:], BF),
            pltpu.VMEM(self_u.shape[1:], BF),
            pltpu.SemaphoreType.DMA((2,)),
        ],
        compiler_params=LIMIT,
        name="selfpart",
    )(*map(onchip, (limits, near, far[2], far[6])), inhbm(self_v[0]), inhbm(self_u[0]))
    partial = pl.pallas_call(
        coupled_kernel,
        out_shape=pltpu.VMEM((angles, window_rows * tile), BF),
        in_specs=[SCALARS] + [ONCHIP] * 5 + [ANYWHERE] * 2,
        out_specs=ONCHIP,
        scratch_shapes=[
            pltpu.VMEM((window_rows, angles, dom_count * link_count * ranks), BF),
            pltpu.VMEM((window_rows, 2, ranks, tile), BF),
            pltpu.VMEM((window_rows, 2, ranks, tile), BF),
            pltpu.SemaphoreType.DMA((2,)),
        ],
        compiler_params=LIMIT,
        name="coupled",
    )(
        link_tiles[0],
        *map(onchip, (limits, arrived, far[4], field, coupling_u[0])),
        inhbm(self_v[0]),
        inhbm(self_u[0]),
    )
    arrived = exchange(partial.reshape(col_count, angles // col_count, window_rows * tile), "col")
    return (incident[0] - arrived.astype(F32).sum(axis=0))[None]


def solution(mesh):
    return jax.shard_map(
        residual,
        mesh=mesh,
        in_specs=(
            P("dom", None, ("col", "row")),
            P("dom", None, "col"),
            P("dom", "row", "col", None, None),
            P("dom", "row", "col", None, None),
            P("dom", "row", "col"),
            P("dom", "row", None, "col", None, None),
            P("dom", "row", None, "col"),
            P("dom", "row", None, "col"),
            P("dom", "col", "row"),
        ),
        out_specs=P("dom", "col", "row"),
        check_vma=False,
    )
```

time: 64.2 us -> 60.4 us (0.941)
  starting transfers between devices: 5.03 us -> 27.7 us
  blocking collectives: 35.7 us -> 17.5 us
  waiting for transfers between devices: 12.1 us -> 6.67 us
  local copies, waits for them, and re-layouts: 2.34 us -> 0.2 us
  Pallas kernels: 7.93 us -> 7.09 us
    all_to_all x2 -> x1, blocking collectives: 35.7 us -> 17.5 us  [exchange(): return lax.all_to_all(value, axis, split_axis=0, concat_axis=0, tiled=True)]
    ppermute x0 -> x4, starting transfers between devices: none -> 12.2 us  [swap(): lax.ppermute(value, axis, [(i, i ^ bits) for i in range(lax.axis_size(axi...]
    all_to_all x1, waiting for transfers between devices: 12.1 us -> 0.01 us  [exchange(): return lax.all_to_all(value, axis, split_axis=0, concat_axis=0, tiled=True)]
    all_to_all x1, starting transfers between devices: 5.03 us -> 15.5 us  [exchange(): return lax.all_to_all(value, axis, split_axis=0, concat_axis=0, tiled=True)]
    ppermute x0 -> x4, waiting for transfers between devices: none -> 6.66 us  [swap(): lax.ppermute(value, axis, [(i, i ^ bits) for i in range(lax.axis_size(axi...]
    squeeze x2, local copies, waits for them, and re-layouts: 1.36 us -> 0.17 us  [the longest x1 0.09 us: residual(): link_tiles[0]]
    unnamed x8 -> x12, local copies, waits for them, and re-layouts: 0.98 us -> 0.03 us
    pallas_call x3 -> x4, Pallas kernels: 7.93 us -> 7.09 us  [the longest x1 2.53 us: residual(): pl.pallas_call(coupled_kernel, out_shape=pltpu.VMEM((angles, window_rows...]
  transfers between devices with their start and end apart: 1 -> 5, of which waited for: 1 -> 3; matrix products, arithmetic and copies ran while one was open for 2% -> 0% of each run, Pallas kernels for 0% -> 4%
where the time goes in v2:
time: 60.4 us; the launch traced here: 60 us
  starting transfers between devices  27.7 us (46%)
  blocking collectives  17.5 us (29%)
  Pallas kernels  7.09 us (12%)
  waiting for transfers between devices  6.67 us (11%)
  other arithmetic  0.66 us (1%)
    all_to_all x1, blocking collectives, exchange(): return lax.all_to_all(value, axis, split_axis=0, concat_axis=0, tiled=True)  17.5 us
    all_to_all x1, starting transfers between devices, exchange(): return lax.all_to_all(value, axis, split_axis=0, concat_axis=0, tiled=True)  15.5 us
    ppermute x4, starting transfers between devices, swap(): lax.ppermute(value, axis, [(i, i ^ bits) for i in range(lax.axis_size(axi...  12.2 us
    ppermute x4, waiting for transfers between devices, swap(): lax.ppermute(value, axis, [(i, i ^ bits) for i in range(lax.axis_size(axi...  6.66 us
    pallas_call x1, Pallas kernels, residual(): pl.pallas_call(coupled_kernel, out_shape=pltpu.VMEM((angles, window_rows...  2.53 us
    pallas_call x1, Pallas kernels, residual(): pl.pallas_call(project_kernel, out_shape=pltpu.VMEM((dom_count * row_coun...  1.99 us
    pallas_call x1, Pallas kernels, residual(): pl.pallas_call(self_kernel, out_shape=pltpu.VMEM((angles, window_rows * t...  1.87 us
  transfers between devices with their start and end apart: 5, of which 3 were waited for; matrix products, arithmetic and copies ran while one was open for 0% of the time, Pallas kernels for 4%

profile of v2, /device:TPU:1, one launch (start us, length us, event | category | flops | bytes accessed | tf_op | source)
XLA Modules:
  0.0 60.0 jit_solution(1684793276489924907)
XLA Ops:
  0.0 0.0 copy-start.2
  0.0 0.0 copy-start.4
  0.0 0.0 copy-start.5
  0.0 0.0 copy-start.1
  0.0 2.0 %project.1 = bf16[64,32,128]{2,1,0:T(8,128)(2,1)} custom-call(bf16[64,512]{1,0:T(8,128)(2,1)} %bitcast.20, bf16[64,4096]{1,0:T(8,128)(2,1)} %bitcast.19), custom_call_target="tpu_custom_call" | custom-call | tf_op jit(solution)/shard_map/project/pallas_call | solution.py:169
  2.0 0.0 copy-start
  2.0 15.5 %all-to-all-start = ((bf16[64,32,128]{2,1,0:T(8,128)(2,1)}), bf16[64,32,128]{2,1,0:T(8,128)(2,1)S(1)}, u32[]{:S(2)}, u32[]{:S(2)}) async-start(bf16[64,32,128]{2,1,0:T(8,128)(2,1)} %project.1), calls=%async_computation | async-start | bytes 1048576 | tf_op jit(solution)/shard_map/all_to_all | solution.py:19
  17.5 0.0 copy-done.2
  17.5 2.9 %collective-permute-start = (bf16[64,512]{1,0:T(8,128)(2,1)S(1)}, bf16[64,512]{1,0:T(8,128)(2,1)S(1)}, u32[]{:S(2)}, u32[]{:S(2)}) collective-permute-start(bf16[64,512]{1,0:T(8,128)(2,1)S(1)} %bitcast.21), channel_id=1, source_target_pairs={{0,8},{8,0},{16,24},{24,16},{32,40},{40,32},{48,56},{56,48},{1,9},... | collective-permute-start | bytes 196616 | tf_op jit(solution)/shard_map/ppermute | solution.py:23
  20.5 4.8 %collective-permute-done = bf16[64,512]{1,0:T(8,128)(2,1)S(1)} collective-permute-done((bf16[64,512]{1,0:T(8,128)(2,1)S(1)}, bf16[64,512]{1,0:T(8,128)(2,1)S(1)}, u32[]{:S(2)}, u32[]{:S(2)}) %collective-permute-start) | collective-permute-done | bytes 65568 | tf_op jit(solution)/shard_map/ppermute | solution.py:23
  25.2 3.1 %collective-permute-start.2 = (bf16[2,64,512]{2,1,0:T(8,128)(2,1)S(1)}, bf16[2,64,512]{2,1,0:T(8,128)(2,1)S(1)}, u32[]{:S(2)}, u32[]{:S(2)}) collective-permute-start(bf16[2,64,512]{2,1,0:T(8,128)(2,1)S(1)} %pad_maximum_fusion.near), channel_id=1, source_target_pairs={{0,16},{8,24},{16,0},{24,8},{32,48},{40,56},{48,32},{56,40},{1,17}... | collective-permute-start | bytes 393224 | tf_op jit(solution)/shard_map/ppermute | solution.py:23
  28.3 3.7 %collective-permute-start.3 = (bf16[2,64,512]{2,1,0:T(8,128)(2,1)S(1)}, bf16[2,64,512]{2,1,0:T(8,128)(2,1)S(1)}, u32[]{:S(2)}, u32[]{:S(2)}) collective-permute-start(bf16[2,64,512]{2,1,0:T(8,128)(2,1)S(1)} %pad_maximum_fusion.near), channel_id=1, source_target_pairs={{0,48},{8,56},{16,32},{24,40},{32,16},{40,24},{48,0},{56,8},{1,49}... | collective-permute-start | bytes 393224 | tf_op jit(solution)/shard_map/ppermute | solution.py:23
  32.0 2.5 %collective-permute-start.1 = (bf16[2,64,512]{2,1,0:T(8,128)(2,1)S(1)}, bf16[2,64,512]{2,1,0:T(8,128)(2,1)S(1)}, u32[]{:S(2)}, u32[]{:S(2)}) collective-permute-start(bf16[2,64,512]{2,1,0:T(8,128)(2,1)S(1)} %pad_maximum_fusion.near), channel_id=1, source_target_pairs={{0,32},{8,40},{16,48},{24,56},{32,0},{40,8},{48,16},{56,24},{1,33}... | collective-permute-start | bytes 393224 | tf_op jit(solution)/shard_map/ppermute | solution.py:23
  34.6 0.0 copy-done.4
  34.6 0.1 copy.11.links
  34.7 0.0 copy-done.5
  34.7 0.1 copy.10.cpl_rank
  34.8 0.0 copy-done.1
  34.8 0.7 %limits.1 = s32[2,12,128]{2,1,0:T(8,128)S(1)} custom-call(s32[2,8]{1,0:T(2,128)S(1)} %bitcast.14, s32[2,8,2]{2,1,0:T(8,128)S(1)} %copy.10.cpl_rank), custom_call_target="tpu_custom_call" | custom-call | tf_op jit(solution)/shard_map/limits/pallas_call | solution.py:187
  35.5 0.0 collective-permute-done.2.far2
  35.5 0.3 collective-permute-done.3.far6
  35.8 1.9 %selfpart.1.field = f32[64,1024]{1,0:T(8,128)S(1)} custom-call(s32[2,12,128]{2,1,0:T(8,128)S(1)} %limits.1, bf16[2,64,512]{2,1,0:T(8,128)(2,1)S(1)} %pad_maximum_fusion.near, bf16[2,64,512]{2,1,0:T(8,128)(2,1)S(1)} %collective-permute-done.2.far2, bf16[2,64,512]{2,1,0:T(8,128)(2,1)S(1)} %collective-permute-done.3.far6, bf16[2,8,64,512]{3,2,1,0:T(8,128)(2,1)} %bitcast.15, ...), custom_call_target="tpu_custom_call" | custom-call | tf_op jit(solution)/shard_map/selfpart/pallas_call | solution.py:195
  37.7 1.6 %collective-permute-done.1.far4 = bf16[2,64,512]{2,1,0:T(8,128)(2,1)S(1)} collective-permute-done((bf16[2,64,512]{2,1,0:T(8,128)(2,1)S(1)}, bf16[2,64,512]{2,1,0:T(8,128)(2,1)S(1)}, u32[]{:S(2)}, u32[]{:S(2)}) %collective-permute-start.1) | collective-permute-done | bytes 131104 | tf_op jit(solution)/shard_map/ppermute | solution.py:23
  39.3 0.0 all-to-all-done.arrived
  39.3 0.0 copy-done
  39.3 0.0 copy-start.3
  39.3 2.5 %coupled.1 = bf16[64,1024]{1,0:T(8,128)(2,1)S(1)} custom-call(s32[2,8,2]{2,1,0:T(8,128)S(1)} %copy.11.links, s32[2,12,128]{2,1,0:T(8,128)S(1)} %limits.1, bf16[64,32,128]{2,1,0:T(8,128)(2,1)S(1)} %all-to-all-done.arrived, bf16[2,64,512]{2,1,0:T(8,128)(2,1)S(1)} %collective-permute-done.1.far4, f32[64,1024]{1,0:T(8,128)S(1)} %selfpart.1.field, ...), custom_call_target="tpu_custom_call" | custom-call | tf_op jit(solution)/shard_map/coupled/pallas_call | solution.py:208
  41.8 17.5 %all_to_all.10 = bf16[8,8,1024]{2,1,0:T(8,128)(2,1)S(1)} all-to-all(bf16[8,8,1024]{2,1,0:T(8,128)(2,1)S(1)} %bitcast.13), channel_id=1, replica_groups=mesh['dom'=8,'row'=8,'col'=8] {'col'}, dimensions={0} | all-to-all | bytes 262144 | tf_op jit(solution)/shard_map/all_to_all | solution.py:19
  59.4 0.0 copy-done.3
  59.4 0.6 %bitcast_subtract_fusion = f32[1,8,1024]{2,1,0:T(8,128)} fusion(f32[1,8,1024]{2,1,0:T(8,128)S(1)} %copy-done.3, f32[8,1024]{1,0:T(8,128)S(1)} %convert_reduce_fusion), kind=kLoop, calls=%fused_computation.2 | loop fusion | flops 8192 | bytes 98304 | tf_op jit(solution)/shard_map/sub | solution.py:228
  (2 shorter events, 0.0 us)
Async XLA Ops:
  0.0 17.5 %copy-start.2 = (bf16[1,64,512]{2,1,0:T(8,128)(2,1)S(1)}, bf16[1,64,512]{2,1,0:T(8,128)(2,1)}, u32[]{:S(2)}) copy-start(bf16[1,64,512]{2,1,0:T(8,128)(2,1)} %param.9) | copy-start | bytes 196612
  0.0 34.6 %copy-start.4 = (s32[1,2,8,2]{2,3,1,0:T(2,128)S(1)}, s32[1,2,8,2]{2,3,1,0:T(2,128)}, u32[]{:S(2)}) copy-start(s32[1,2,8,2]{2,3,1,0:T(2,128)} %param.16) | copy-start | bytes 388
  0.0 34.7 %copy-start.5 = (s32[1,2,8,2]{2,3,1,0:T(2,128)S(1)}, s32[1,2,8,2]{2,3,1,0:T(2,128)}, u32[]{:S(2)}) copy-start(s32[1,2,8,2]{2,3,1,0:T(2,128)} %param.15) | copy-start | bytes 388
  0.0 34.8 %copy-start.1 = (s32[1,2,8]{2,1,0:T(2,128)S(1)}, s32[1,2,8]{2,1,0:T(2,128)}, u32[]{:S(2)}) copy-start(s32[1,2,8]{2,1,0:T(2,128)} %param.13) | copy-start | bytes 196
  2.0 37.2 %copy-start = (bf16[1,2,8,2,64,512]{5,4,3,2,1,0:T(8,128)(2,1)S(1)}, bf16[1,2,8,2,64,512]{5,4,3,2,1,0:T(8,128)(2,1)}, u32[]{:S(2)}) copy-start(bf16[1,2,8,2,64,512]{5,4,3,2,1,0:T(8,128)(2,1)} %param.14) | copy-start | bytes 6291460
  2.0 37.2 %all-to-all-start = ((bf16[64,32,128]{2,1,0:T(8,128)(2,1)}), bf16[64,32,128]{2,1,0:T(8,128)(2,1)S(1)}, u32[]{:S(2)}, u32[]{:S(2)}) async-start(bf16[64,32,128]{2,1,0:T(8,128)(2,1)} %project.1), calls=%async_computation | async-start | bytes 1048576 | tf_op jit(solution)/shard_map/all_to_all | solution.py:19
  17.5 7.7 %collective-permute-start = (bf16[64,512]{1,0:T(8,128)(2,1)S(1)}, bf16[64,512]{1,0:T(8,128)(2,1)S(1)}, u32[]{:S(2)}, u32[]{:S(2)}) collective-permute-start(bf16[64,512]{1,0:T(8,128)(2,1)S(1)} %bitcast.21), channel_id=1, source_target_pairs={{0,8},{8,0},{16,24},{24,16},{32,40},{40,32},{48,56},{56,48},{1,9},... | collective-permute-start | bytes 196616 | tf_op jit(solution)/shard_map/ppermute | solution.py:23
  25.2 10.2 %collective-permute-start.2 = (bf16[2,64,512]{2,1,0:T(8,128)(2,1)S(1)}, bf16[2,64,512]{2,1,0:T(8,128)(2,1)S(1)}, u32[]{:S(2)}, u32[]{:S(2)}) collective-permute-start(bf16[2,64,512]{2,1,0:T(8,128)(2,1)S(1)} %pad_maximum_fusion.near), channel_id=1, source_target_pairs={{0,16},{8,24},{16,0},{24,8},{32,48},{40,56},{48,32},{56,40},{1,17}... | collective-permute-start | bytes 393224 | tf_op jit(solution)/shard_map/ppermute | solution.py:23
  28.3 7.5 %collective-permute-start.3 = (bf16[2,64,512]{2,1,0:T(8,128)(2,1)S(1)}, bf16[2,64,512]{2,1,0:T(8,128)(2,1)S(1)}, u32[]{:S(2)}, u32[]{:S(2)}) collective-permute-start(bf16[2,64,512]{2,1,0:T(8,128)(2,1)S(1)} %pad_maximum_fusion.near), channel_id=1, source_target_pairs={{0,48},{8,56},{16,32},{24,40},{32,16},{40,24},{48,0},{56,8},{1,49}... | collective-permute-start | bytes 393224 | tf_op jit(solution)/shard_map/ppermute | solution.py:23
  32.0 7.2 %collective-permute-start.1 = (bf16[2,64,512]{2,1,0:T(8,128)(2,1)S(1)}, bf16[2,64,512]{2,1,0:T(8,128)(2,1)S(1)}, u32[]{:S(2)}, u32[]{:S(2)}) collective-permute-start(bf16[2,64,512]{2,1,0:T(8,128)(2,1)S(1)} %pad_maximum_fusion.near), channel_id=1, source_target_pairs={{0,32},{8,40},{16,48},{24,56},{32,0},{40,8},{48,16},{56,24},{1,33}... | collective-permute-start | bytes 393224 | tf_op jit(solution)/shard_map/ppermute | solution.py:23
  39.3 20.1 %copy-start.3 = (f32[1,8,1024]{2,1,0:T(8,128)S(1)}, f32[1,8,1024]{2,1,0:T(8,128)}, u32[]{:S(2)}) copy-start(f32[1,8,1024]{2,1,0:T(8,128)} %param.17) | copy-start | bytes 98308

commit v3 on v2

--- a/solution.py
+++ b/solution.py
@@ -85,36 +85,41 @@
     return jnp.where(low_lanes(shape), level, level - shape[1] // 2)
 
 
-def self_kernel(limits, near, far2, far6, v_hbm, u_hbm, out, v, u, arrivals):
-    rows, _, ranks, tile = v.shape
-    fetch = [
-        pltpu.make_async_copy(src, dst, arrivals.at[i])
-        for i, (src, dst) in enumerate(((v_hbm, v), (u_hbm, u)))
-    ]
+def self_kernel(slots, limits, currents, v_hbm, u_hbm, out, v, u, arrivals, before=None):
+    rows, ranks, tile = v.shape[1], v.shape[3], v.shape[4]
+    fetch = []
+    for src, dst in ((v_hbm, v), (u_hbm, u)):
+        for i, slot in enumerate(slots):
+            pair = pl.ds(2 * pair_of(slot), 2)
+            fetch.append(
+                pltpu.make_async_copy(src.at[:, pair], dst.at[i], arrivals.at[len(fetch)])
+            )
     for copy in fetch:
         copy.start()
-    fetch[0].wait()
-    slots = ((0, near), (1, far2), (3, far6))
-    left = []
-    for t in range(rows):
-        for slot, currents in slots:
-            pair = pair_of(slot)
-            left.append(
-                projected(currents, v[t, pl.ds(2 * pair, 2)], limits[t, pl.ds(pair, 1)])
-            )
-    fetch[1].wait()
-    for t in range(rows):
-        total = None
-        for i, (slot, _) in enumerate(slots):
-            factors = u[t, pl.ds(2 * pair_of(slot), 2)].reshape(2 * ranks, tile)
-            part = jnp.dot(left[t * len(slots) + i], factors, preferred_element_type=F32)
-            total = part if total is None else total + part
-        out[:, t * tile : (t + 1) * tile] = total
-
-
-def coupled_kernel(
-    links, limits, arrived, far4, field, cu, v_hbm, u_hbm, out, picked, last_v, last_u, arrivals
-):
+    left = {}
+    for i, slot in enumerate(slots):
+        fetch[i].wait()
+        for t in range(rows):
+            left[t, i] = projected(currents[i], v[i, t], limits[t, pl.ds(pair_of(slot), 1)])
+    for copy in fetch[len(slots) :]:
+        copy.wait()
+    for t in range(rows):
+        at = slice(t * tile, (t + 1) * tile)
+        weights = jnp.concatenate([left[t, i] for i in range(len(slots))], axis=1)
+        factors = jnp.concatenate([u[i, t].reshape(2 * ranks, tile) for i in range(len(slots))], axis=0)
+        total = jnp.dot(weights, factors, preferred_element_type=F32)
+        out[:, at] = total if before is None else before[:, at] + total
+
+
+def self_first_kernel(limits, near, far4, v_hbm, u_hbm, out, v, u, arrivals):
+    self_kernel((0, 2), limits, (near, far4), v_hbm, u_hbm, out, v, u, arrivals)
+
+
+def self_second_kernel(limits, far2, far6, before, v_hbm, u_hbm, out, v, u, arrivals):
+    self_kernel((1, 3), limits, (far2, far6), v_hbm, u_hbm, out, v, u, arrivals, before)
+
+
+def coupled_kernel(links, limits, arrived, field, cu, out, picked):
     rows, parts, link_count, ranks, tile = cu.shape
     angles = field.shape[0]
     half, lanes = arrived.shape[1:]
@@ -122,13 +127,6 @@
     pairs = limits.shape[1] - parts
     low = low_lanes((half, lanes))
     level = levels((angles, lanes))
-    last = pl.ds(2 * pair_of(2), 2)
-    fetch = [
-        pltpu.make_async_copy(src.at[:, last], dst, arrivals.at[i])
-        for i, (src, dst) in enumerate(((v_hbm, last_v), (u_hbm, last_u)))
-    ]
-    for copy in fetch:
-        copy.start()
     for t in range(rows):
         for e in range(parts):
             one = arrived[e * block_tiles + links[t, e, 0]].astype(F32)
@@ -138,19 +136,9 @@
             value = jnp.concatenate([top, bottom], axis=0)
             value = jnp.where(level < limits[t, pairs + e : pairs + e + 1], value, 0.0)
             picked[t, :, e * lanes : (e + 1) * lanes] = value.astype(BF)
-    totals = []
-    for t in range(rows):
-        total = field[:, t * tile : (t + 1) * tile]
-        total += jnp.dot(
+    for t in range(rows):
+        total = field[:, t * tile : (t + 1) * tile] + jnp.dot(
             picked[t], cu[t].reshape(parts * link_count * ranks, tile), preferred_element_type=F32
-        )
-        totals.append(total)
-    for copy in fetch:
-        copy.wait()
-    for t in range(rows):
-        left = projected(far4, last_v[t], limits[t, pl.ds(pair_of(2), 1)])
-        total = totals[t] + jnp.dot(
-            left, last_u[t].reshape(lanes, tile), preferred_element_type=F32
         )
         out[:, t * tile : (t + 1) * tile] = total.astype(out.dtype)
 
@@ -182,7 +170,7 @@
     arrived = exchange(outgoing, ("dom", "row"))
     near = jnp.stack([own, neighbour])
     far = {}
-    for bits in (2, 6, 4):
+    for bits in (4, 2, 6):
         far[bits] = swap(near, "row", bits)
     limits = pl.pallas_call(
         limits_kernel,
@@ -192,38 +180,35 @@
         compiler_params=LIMIT,
         name="limits",
     )(self_rank[0], coupling_rank[0])
-    field = pl.pallas_call(
-        self_kernel,
-        out_shape=pltpu.VMEM((angles, window_rows * tile), F32),
-        in_specs=[ONCHIP] * 4 + [ANYWHERE] * 2,
-        out_specs=ONCHIP,
-        scratch_shapes=[
-            pltpu.VMEM(self_v.shape[1:], BF),
-            pltpu.VMEM(self_u.shape[1:], BF),
-            pltpu.SemaphoreType.DMA((2,)),
-        ],
-        compiler_params=LIMIT,
-        name="selfpart",
-    )(*map(onchip, (limits, near, far[2], far[6])), inhbm(self_v[0]), inhbm(self_u[0]))
+    field = ()
+    for kernel, currents_in in (
+        (self_first_kernel, (near, far[4])), (self_second_kernel, (far[2], far[6]))
+    ):
+        onchip_in = (limits, *currents_in, *field)
+        pair_block = (2, window_rows, 2, ranks, tile)
+        field = (
+            pl.pallas_call(
+                kernel,
+                out_shape=pltpu.VMEM((angles, window_rows * tile), F32),
+                in_specs=[ONCHIP] * len(onchip_in) + [ANYWHERE] * 2,
+                out_specs=ONCHIP,
+                scratch_shapes=[
+                    pltpu.VMEM(pair_block, BF),
+                    pltpu.VMEM(pair_block, BF),
+                    pltpu.SemaphoreType.DMA((4,)),
+                ],
+                compiler_params=LIMIT,
+            )(*map(onchip, onchip_in), inhbm(self_v[0]), inhbm(self_u[0])),
+        )
     partial = pl.pallas_call(
         coupled_kernel,
         out_shape=pltpu.VMEM((angles, window_rows * tile), BF),
-        in_specs=[SCALARS] + [ONCHIP] * 5 + [ANYWHERE] * 2,
+        in_specs=[SCALARS] + [ONCHIP] * 4,
         out_specs=ONCHIP,
-        scratch_shapes=[
-            pltpu.VMEM((window_rows, angles, dom_count * link_count * ranks), BF),
-            pltpu.VMEM((window_rows, 2, ranks, tile), BF),
-            pltpu.VMEM((window_rows, 2, ranks, tile), BF),
-            pltpu.SemaphoreType.DMA((2,)),
-        ],
+        scratch_shapes=[pltpu.VMEM((window_rows, angles, dom_count * link_count * ranks), BF)],
         compiler_params=LIMIT,
         name="coupled",
-    )(
-        link_tiles[0],
-        *map(onchip, (limits, arrived, far[4], field, coupling_u[0])),
-        inhbm(self_v[0]),
-        inhbm(self_u[0]),
-    )
+    )(link_tiles[0], *map(onchip, (limits, arrived, *field, coupling_u[0])))
     arrived = exchange(partial.reshape(col_count, angles // col_count, window_rows * tile), "col")
     return (incident[0] - arrived.astype(F32).sum(axis=0))[None]
 

time: 60.4 us -> 60.3 us (level)
    pallas_call x1 -> x2, Pallas kernels: 1.87 us -> 3.32 us  [residual(): pl.pallas_call(kernel, out_shape=pltpu.VMEM((angles, window_rows * tile),...]
    pallas_call x1, Pallas kernels: 2.53 us -> 1.2 us  [residual(): pl.pallas_call(coupled_kernel, out_shape=pltpu.VMEM((angles, window_rows...]
  transfers between devices with their start and end apart: 5 -> 5, of which waited for: 3 -> 2; matrix products, arithmetic and copies ran while one was open for 0% -> 0% of each run, Pallas kernels for 4% -> 7%
where the time goes in v3:
time: 60.3 us; the launch traced here: 59.9 us
  starting transfers between devices  27.6 us (46%)
  blocking collectives  17.5 us (29%)
  Pallas kernels  7.21 us (12%)
  waiting for transfers between devices  6.56 us (11%)
  other arithmetic  0.66 us (1%)
    all_to_all x1, blocking collectives, exchange(): return lax.all_to_all(value, axis, split_axis=0, concat_axis=0, tiled=True)  17.5 us
    all_to_all x1, starting transfers between devices, exchange(): return lax.all_to_all(value, axis, split_axis=0, concat_axis=0, tiled=True)  15.3 us
    ppermute x4, starting transfers between devices, swap(): lax.ppermute(value, axis, [(i, i ^ bits) for i in range(lax.axis_size(axi...  12.2 us
    ppermute x4, waiting for transfers between devices, swap(): lax.ppermute(value, axis, [(i, i ^ bits) for i in range(lax.axis_size(axi...  6.56 us
    pallas_call x2, Pallas kernels, residual(): pl.pallas_call(kernel, out_shape=pltpu.VMEM((angles, window_rows * tile),...  3.32 us
    pallas_call x1, Pallas kernels, residual(): pl.pallas_call(project_kernel, out_shape=pltpu.VMEM((dom_count * row_coun...  1.99 us
  transfers between devices with their start and end apart: 5, of which 2 were waited for; matrix products, arithmetic and copies ran while one was open for 0% of the time, Pallas kernels for 7%

profile of v3, /device:TPU:1, one launch (start us, length us, event | category | flops | bytes accessed | tf_op | source)
XLA Modules:
  0.0 59.9 jit_solution(5617366203731658939)
XLA Ops:
  0.0 0.0 copy-start.2
  0.0 0.0 copy-start.4
  0.0 0.0 copy-start.5
  0.0 0.0 copy-start.1
  0.0 2.0 %project.1 = bf16[64,32,128]{2,1,0:T(8,128)(2,1)} custom-call(bf16[64,512]{1,0:T(8,128)(2,1)} %bitcast.20, bf16[64,4096]{1,0:T(8,128)(2,1)} %bitcast.19), custom_call_target="tpu_custom_call" | custom-call | tf_op jit(solution)/shard_map/project/pallas_call | solution.py:157
  2.0 15.3 %all-to-all-start = ((bf16[64,32,128]{2,1,0:T(8,128)(2,1)}), bf16[64,32,128]{2,1,0:T(8,128)(2,1)S(1)}, u32[]{:S(2)}, u32[]{:S(2)}) async-start(bf16[64,32,128]{2,1,0:T(8,128)(2,1)} %project.1), calls=%async_computation | async-start | bytes 1048576 | tf_op jit(solution)/shard_map/all_to_all | solution.py:19
  17.4 0.0 copy-done.2
  17.4 2.9 %collective-permute-start = (bf16[64,512]{1,0:T(8,128)(2,1)S(1)}, bf16[64,512]{1,0:T(8,128)(2,1)S(1)}, u32[]{:S(2)}, u32[]{:S(2)}) collective-permute-start(bf16[64,512]{1,0:T(8,128)(2,1)S(1)} %bitcast.21), channel_id=1, source_target_pairs={{0,8},{8,0},{16,24},{24,16},{32,40},{40,32},{48,56},{56,48},{1,9},... | collective-permute-start | bytes 196616 | tf_op jit(solution)/shard_map/ppermute | solution.py:23
  20.3 4.8 %collective-permute-done = bf16[64,512]{1,0:T(8,128)(2,1)S(1)} collective-permute-done((bf16[64,512]{1,0:T(8,128)(2,1)S(1)}, bf16[64,512]{1,0:T(8,128)(2,1)S(1)}, u32[]{:S(2)}, u32[]{:S(2)}) %collective-permute-start) | collective-permute-done | bytes 65568 | tf_op jit(solution)/shard_map/ppermute | solution.py:23
  25.1 4.6 %collective-permute-start.3 = (bf16[2,64,512]{2,1,0:T(8,128)(2,1)S(1)}, bf16[2,64,512]{2,1,0:T(8,128)(2,1)S(1)}, u32[]{:S(2)}, u32[]{:S(2)}) collective-permute-start(bf16[2,64,512]{2,1,0:T(8,128)(2,1)S(1)} %pad_maximum_fusion.near), channel_id=1, source_target_pairs={{0,32},{8,40},{16,48},{24,56},{32,0},{40,8},{48,16},{56,24},{1,33}... | collective-permute-start | bytes 393224 | tf_op jit(solution)/shard_map/ppermute | solution.py:23
  29.7 2.2 %collective-permute-start.1 = (bf16[2,64,512]{2,1,0:T(8,128)(2,1)S(1)}, bf16[2,64,512]{2,1,0:T(8,128)(2,1)S(1)}, u32[]{:S(2)}, u32[]{:S(2)}) collective-permute-start(bf16[2,64,512]{2,1,0:T(8,128)(2,1)S(1)} %pad_maximum_fusion.near), channel_id=1, source_target_pairs={{0,16},{8,24},{16,0},{24,8},{32,48},{40,56},{48,32},{56,40},{1,17}... | collective-permute-start | bytes 393224 | tf_op jit(solution)/shard_map/ppermute | solution.py:23
  31.9 2.5 %collective-permute-start.2 = (bf16[2,64,512]{2,1,0:T(8,128)(2,1)S(1)}, bf16[2,64,512]{2,1,0:T(8,128)(2,1)S(1)}, u32[]{:S(2)}, u32[]{:S(2)}) collective-permute-start(bf16[2,64,512]{2,1,0:T(8,128)(2,1)S(1)} %pad_maximum_fusion.near), channel_id=1, source_target_pairs={{0,48},{8,56},{16,32},{24,40},{32,16},{40,24},{48,0},{56,8},{1,49}... | collective-permute-start | bytes 393224 | tf_op jit(solution)/shard_map/ppermute | solution.py:23
  34.4 0.0 copy-done.4
  34.4 0.1 copy.11.links
  34.5 0.0 copy-done.5
  34.5 0.1 copy.10.cpl_rank
  34.6 0.0 copy-done.1
  34.6 0.7 %limits.1 = s32[2,12,128]{2,1,0:T(8,128)S(1)} custom-call(s32[2,8]{1,0:T(2,128)S(1)} %bitcast.14, s32[2,8,2]{2,1,0:T(8,128)S(1)} %copy.10.cpl_rank), custom_call_target="tpu_custom_call" | custom-call | tf_op jit(solution)/shard_map/limits/pallas_call | solution.py:175
  35.3 0.0 collective-permute-done.3.far4
  35.3 1.7 %shard_map.91.before = f32[64,1024]{1,0:T(8,128)S(1)} custom-call(s32[2,12,128]{2,1,0:T(8,128)S(1)} %limits.1, bf16[2,64,512]{2,1,0:T(8,128)(2,1)S(1)} %pad_maximum_fusion.near, bf16[2,64,512]{2,1,0:T(8,128)(2,1)S(1)} %collective-permute-done.3.far4, bf16[2,8,64,512]{3,2,1,0:T(8,128)(2,1)} %bitcast.15, bf16[2,8,64,512]{3,2,1,0:T(8,128)(2,1)} %bitcast.17), custom_call_target="tpu_custom_call" | custom-call | tf_op jit(solution)/shard_map/pallas_call | solution.py:190
  37.0 0.0 copy-start
  37.0 0.0 collective-permute-done.1.far2
  37.0 1.8 %collective-permute-done.2.far6 = bf16[2,64,512]{2,1,0:T(8,128)(2,1)S(1)} collective-permute-done((bf16[2,64,512]{2,1,0:T(8,128)(2,1)S(1)}, bf16[2,64,512]{2,1,0:T(8,128)(2,1)S(1)}, u32[]{:S(2)}, u32[]{:S(2)}) %collective-permute-start.2) | collective-permute-done | bytes 131104 | tf_op jit(solution)/shard_map/ppermute | solution.py:23
  38.8 1.7 %shard_map.92.field = f32[64,1024]{1,0:T(8,128)S(1)} custom-call(s32[2,12,128]{2,1,0:T(8,128)S(1)} %limits.1, bf16[2,64,512]{2,1,0:T(8,128)(2,1)S(1)} %collective-permute-done.1.far2, bf16[2,64,512]{2,1,0:T(8,128)(2,1)S(1)} %collective-permute-done.2.far6, f32[64,1024]{1,0:T(8,128)S(1)} %shard_map.91.before, bf16[2,8,64,512]{3,2,1,0:T(8,128)(2,1)} %bitcast.16, ...), custom_call_target="tpu_custom_call" | custom-call | tf_op jit(solution)/shard_map/pallas_call | solution.py:190
  40.5 0.0 copy-start.3
  40.5 0.0 all-to-all-done.arrived
  40.5 0.0 copy-done
  40.5 1.2 %coupled.1 = bf16[64,1024]{1,0:T(8,128)(2,1)S(1)} custom-call(s32[2,8,2]{2,1,0:T(8,128)S(1)} %copy.11.links, s32[2,12,128]{2,1,0:T(8,128)S(1)} %limits.1, bf16[64,32,128]{2,1,0:T(8,128)(2,1)S(1)} %all-to-all-done.arrived, f32[64,1024]{1,0:T(8,128)S(1)} %shard_map.92.field, bf16[2,8,2,64,512]{4,3,2,1,0:T(8,128)(2,1)S(1)} %bitcast.12), custom_call_target="tpu_custom_call" | custom-call | tf_op jit(solution)/shard_map/coupled/pallas_call | solution.py:203
  41.7 17.5 %all_to_all.10 = bf16[8,8,1024]{2,1,0:T(8,128)(2,1)S(1)} all-to-all(bf16[8,8,1024]{2,1,0:T(8,128)(2,1)S(1)} %bitcast.13), channel_id=1, replica_groups=mesh['dom'=8,'row'=8,'col'=8] {'col'}, dimensions={0} | all-to-all | bytes 262144 | tf_op jit(solution)/shard_map/all_to_all | solution.py:19
  59.3 0.0 copy-done.3
  59.3 0.6 %bitcast_subtract_fusion = f32[1,8,1024]{2,1,0:T(8,128)} fusion(f32[1,8,1024]{2,1,0:T(8,128)S(1)} %copy-done.3, f32[8,1024]{1,0:T(8,128)S(1)} %convert_reduce_fusion), kind=kLoop, calls=%fused_computation.2 | loop fusion | flops 8192 | bytes 98304 | tf_op jit(solution)/shard_map/sub | solution.py:213
  (2 shorter events, 0.0 us)
Async XLA Ops:
  0.0 17.4 %copy-start.2 = (bf16[1,64,512]{2,1,0:T(8,128)(2,1)S(1)}, bf16[1,64,512]{2,1,0:T(8,128)(2,1)}, u32[]{:S(2)}) copy-start(bf16[1,64,512]{2,1,0:T(8,128)(2,1)} %param.9) | copy-start | bytes 196612
  0.0 34.4 %copy-start.4 = (s32[1,2,8,2]{2,3,1,0:T(2,128)S(1)}, s32[1,2,8,2]{2,3,1,0:T(2,128)}, u32[]{:S(2)}) copy-start(s32[1,2,8,2]{2,3,1,0:T(2,128)} %param.16) | copy-start | bytes 388
  0.0 34.5 %copy-start.5 = (s32[1,2,8,2]{2,3,1,0:T(2,128)S(1)}, s32[1,2,8,2]{2,3,1,0:T(2,128)}, u32[]{:S(2)}) copy-start(s32[1,2,8,2]{2,3,1,0:T(2,128)} %param.15) | copy-start | bytes 388
  0.0 34.6 %copy-start.1 = (s32[1,2,8]{2,1,0:T(2,128)S(1)}, s32[1,2,8]{2,1,0:T(2,128)}, u32[]{:S(2)}) copy-start(s32[1,2,8]{2,1,0:T(2,128)} %param.13) | copy-start | bytes 196
  2.0 38.5 %all-to-all-start = ((bf16[64,32,128]{2,1,0:T(8,128)(2,1)}), bf16[64,32,128]{2,1,0:T(8,128)(2,1)S(1)}, u32[]{:S(2)}, u32[]{:S(2)}) async-start(bf16[64,32,128]{2,1,0:T(8,128)(2,1)} %project.1), calls=%async_computation | async-start | bytes 1048576 | tf_op jit(solution)/shard_map/all_to_all | solution.py:19
  17.4 7.7 %collective-permute-start = (bf16[64,512]{1,0:T(8,128)(2,1)S(1)}, bf16[64,512]{1,0:T(8,128)(2,1)S(1)}, u32[]{:S(2)}, u32[]{:S(2)}) collective-permute-start(bf16[64,512]{1,0:T(8,128)(2,1)S(1)} %bitcast.21), channel_id=1, source_target_pairs={{0,8},{8,0},{16,24},{24,16},{32,40},{40,32},{48,56},{56,48},{1,9},... | collective-permute-start | bytes 196616 | tf_op jit(solution)/shard_map/ppermute | solution.py:23
  25.1 10.2 %collective-permute-start.3 = (bf16[2,64,512]{2,1,0:T(8,128)(2,1)S(1)}, bf16[2,64,512]{2,1,0:T(8,128)(2,1)S(1)}, u32[]{:S(2)}, u32[]{:S(2)}) collective-permute-start(bf16[2,64,512]{2,1,0:T(8,128)(2,1)S(1)} %pad_maximum_fusion.near), channel_id=1, source_target_pairs={{0,32},{8,40},{16,48},{24,56},{32,0},{40,8},{48,16},{56,24},{1,33}... | collective-permute-start | bytes 393224 | tf_op jit(solution)/shard_map/ppermute | solution.py:23
  29.7 7.3 %collective-permute-start.1 = (bf16[2,64,512]{2,1,0:T(8,128)(2,1)S(1)}, bf16[2,64,512]{2,1,0:T(8,128)(2,1)S(1)}, u32[]{:S(2)}, u32[]{:S(2)}) collective-permute-start(bf16[2,64,512]{2,1,0:T(8,128)(2,1)S(1)} %pad_maximum_fusion.near), channel_id=1, source_target_pairs={{0,16},{8,24},{16,0},{24,8},{32,48},{40,56},{48,32},{56,40},{1,17}... | collective-permute-start | bytes 393224 | tf_op jit(solution)/shard_map/ppermute | solution.py:23
  31.9 6.9 %collective-permute-start.2 = (bf16[2,64,512]{2,1,0:T(8,128)(2,1)S(1)}, bf16[2,64,512]{2,1,0:T(8,128)(2,1)S(1)}, u32[]{:S(2)}, u32[]{:S(2)}) collective-permute-start(bf16[2,64,512]{2,1,0:T(8,128)(2,1)S(1)} %pad_maximum_fusion.near), channel_id=1, source_target_pairs={{0,48},{8,56},{16,32},{24,40},{32,16},{40,24},{48,0},{56,8},{1,49}... | collective-permute-start | bytes 393224 | tf_op jit(solution)/shard_map/ppermute | solution.py:23
  37.0 3.5 %copy-start = (bf16[1,2,8,2,64,512]{5,4,3,2,1,0:T(8,128)(2,1)S(1)}, bf16[1,2,8,2,64,512]{5,4,3,2,1,0:T(8,128)(2,1)}, u32[]{:S(2)}) copy-start(bf16[1,2,8,2,64,512]{5,4,3,2,1,0:T(8,128)(2,1)} %param.14) | copy-start | bytes 6291460
  40.5 18.8 %copy-start.3 = (f32[1,8,1024]{2,1,0:T(8,128)S(1)}, f32[1,8,1024]{2,1,0:T(8,128)}, u32[]{:S(2)}) copy-start(f32[1,8,1024]{2,1,0:T(8,128)} %param.17) | copy-start | bytes 98308

commit v4 on v3

--- a/solution.py
+++ b/solution.py
@@ -10,7 +10,6 @@
 F32 = jnp.float32
 NT = (((1,), (1,)), ((), ()))
 ONCHIP = pl.BlockSpec(memory_space=pltpu.VMEM)
-SCALARS = pl.BlockSpec(memory_space=pltpu.SMEM)
 ANYWHERE = pl.BlockSpec(memory_space=pl.ANY)
 LIMIT = pltpu.CompilerParams(vmem_limit_bytes=16 * 2**20)
 
@@ -57,11 +56,12 @@
     rows, pairs = self_rank.shape[0], self_rank.shape[1] // 2
     low = low_lanes((1, out.shape[-1]))
     for t in range(rows):
+        own = self_rank[t : t + 1, :]
         for q in range(pairs):
-            out[t, q : q + 1] = jnp.where(low, self_rank[t, 2 * q], self_rank[t, 2 * q + 1])
+            out[t, q : q + 1] = jnp.where(low, own[0, 2 * q], own[0, 2 * q + 1])
         for e in range(cpl_rank.shape[1]):
-            at = pairs + e
-            out[t, at : at + 1] = jnp.where(low, cpl_rank[t, e, 0], cpl_rank[t, e, 1])
+            pair = cpl_rank[t, e : e + 1, :]
+            out[t, pairs + e : pairs + e + 1] = jnp.where(low, pair[0, 0], pair[0, 1])
 
 
 def pair_of(slot):
@@ -129,8 +129,9 @@
     level = levels((angles, lanes))
     for t in range(rows):
         for e in range(parts):
-            one = arrived[e * block_tiles + links[t, e, 0]].astype(F32)
-            two = arrived[e * block_tiles + links[t, e, 1]].astype(F32)
+            link = links[t, e : e + 1, :]
+            one = arrived[e * block_tiles + link[0, 0]].astype(F32)
+            two = arrived[e * block_tiles + link[0, 1]].astype(F32)
             top = jnp.where(low, one, pltpu.roll(two, ranks, 1))
             bottom = jnp.where(low, pltpu.roll(one, ranks, 1), two)
             value = jnp.concatenate([top, bottom], axis=0)
@@ -170,16 +171,16 @@
     arrived = exchange(outgoing, ("dom", "row"))
     near = jnp.stack([own, neighbour])
     far = {}
-    for bits in (4, 2, 6):
+    for bits in (4, 6, 2):
         far[bits] = swap(near, "row", bits)
     limits = pl.pallas_call(
         limits_kernel,
         out_shape=pltpu.VMEM((window_rows, tiles // 2 + dom_count, 2 * ranks), jnp.int32),
-        in_specs=[SCALARS, SCALARS],
+        in_specs=[ONCHIP, ONCHIP],
         out_specs=ONCHIP,
         compiler_params=LIMIT,
         name="limits",
-    )(self_rank[0], coupling_rank[0])
+    )(onchip(self_rank[0]), onchip(coupling_rank[0]))
     field = ()
     for kernel, currents_in in (
         (self_first_kernel, (near, far[4])), (self_second_kernel, (far[2], far[6]))
@@ -203,12 +204,12 @@
     partial = pl.pallas_call(
         coupled_kernel,
         out_shape=pltpu.VMEM((angles, window_rows * tile), BF),
-        in_specs=[SCALARS] + [ONCHIP] * 4,
+        in_specs=[ONCHIP] * 5,
         out_specs=ONCHIP,
         scratch_shapes=[pltpu.VMEM((window_rows, angles, dom_count * link_count * ranks), BF)],
         compiler_params=LIMIT,
         name="coupled",
-    )(link_tiles[0], *map(onchip, (limits, arrived, *field, coupling_u[0])))
+    )(*map(onchip, (link_tiles[0], limits, arrived, *field, coupling_u[0])))
     arrived = exchange(partial.reshape(col_count, angles // col_count, window_rows * tile), "col")
     return (incident[0] - arrived.astype(F32).sum(axis=0))[None]
 

time: 60.3 us -> 59.8 us (level)
  Pallas kernels: 7.21 us -> 6.16 us
  transfers between devices with their start and end apart: 5 -> 5, of which waited for: 2 -> 2; matrix products, arithmetic and copies ran while one was open for 0% -> 0% of each run, Pallas kernels for 7% -> 6%
where the time goes in v4:
time: 59.8 us; the launch traced here: 59.4 us
  starting transfers between devices  27.6 us (46%)
  blocking collectives  17.5 us (29%)
  waiting for transfers between devices  7.12 us (12%)
  Pallas kernels  6.16 us (10%)
  other arithmetic  0.66 us (1%)
    all_to_all x1, blocking collectives, exchange(): return lax.all_to_all(value, axis, split_axis=0, concat_axis=0, tiled=True)  17.5 us
    all_to_all x1, starting transfers between devices, exchange(): return lax.all_to_all(value, axis, split_axis=0, concat_axis=0, tiled=True)  15.3 us
    ppermute x4, starting transfers between devices, swap(): lax.ppermute(value, axis, [(i, i ^ bits) for i in range(lax.axis_size(axi...  12.2 us
    ppermute x4, waiting for transfers between devices, swap(): lax.ppermute(value, axis, [(i, i ^ bits) for i in range(lax.axis_size(axi...  7.12 us
    pallas_call x2, Pallas kernels, residual(): pl.pallas_call(kernel, out_shape=pltpu.VMEM((angles, window_rows * tile),...  3.32 us
    pallas_call x1, Pallas kernels, residual(): pl.pallas_call(project_kernel, out_shape=pltpu.VMEM((dom_count * row_coun...  1.99 us
  transfers between devices with their start and end apart: 5, of which 2 were waited for; matrix products, arithmetic and copies ran while one was open for 0% of the time, Pallas kernels for 6%

profile of v4, /device:TPU:1, one launch (start us, length us, event | category | flops | bytes accessed | tf_op | source)
XLA Modules:
  0.0 59.4 jit_solution(11739269599846404992)
XLA Ops:
  0.0 0.0 copy-start.2
  0.0 0.0 copy-start.4
  0.0 0.0 copy-start.5
  0.0 0.0 copy-start.1
  0.0 2.0 %project.1 = bf16[64,32,128]{2,1,0:T(8,128)(2,1)} custom-call(bf16[64,512]{1,0:T(8,128)(2,1)} %bitcast.20, bf16[64,4096]{1,0:T(8,128)(2,1)} %bitcast.19), custom_call_target="tpu_custom_call" | custom-call | tf_op jit(solution)/shard_map/project/pallas_call | solution.py:158
  2.0 15.3 %all-to-all-start = ((bf16[64,32,128]{2,1,0:T(8,128)(2,1)}), bf16[64,32,128]{2,1,0:T(8,128)(2,1)S(1)}, u32[]{:S(2)}, u32[]{:S(2)}) async-start(bf16[64,32,128]{2,1,0:T(8,128)(2,1)} %project.1), calls=%async_computation | async-start | bytes 1048576 | tf_op jit(solution)/shard_map/all_to_all | solution.py:18
  17.4 0.0 copy-done.2
  17.4 2.9 %collective-permute-start = (bf16[64,512]{1,0:T(8,128)(2,1)S(1)}, bf16[64,512]{1,0:T(8,128)(2,1)S(1)}, u32[]{:S(2)}, u32[]{:S(2)}) collective-permute-start(bf16[64,512]{1,0:T(8,128)(2,1)S(1)} %bitcast.21), channel_id=1, source_target_pairs={{0,8},{8,0},{16,24},{24,16},{32,40},{40,32},{48,56},{56,48},{1,9},... | collective-permute-start | bytes 196616 | tf_op jit(solution)/shard_map/ppermute | solution.py:22
  20.3 4.8 %collective-permute-done = bf16[64,512]{1,0:T(8,128)(2,1)S(1)} collective-permute-done((bf16[64,512]{1,0:T(8,128)(2,1)S(1)}, bf16[64,512]{1,0:T(8,128)(2,1)S(1)}, u32[]{:S(2)}, u32[]{:S(2)}) %collective-permute-start) | collective-permute-done | bytes 65568 | tf_op jit(solution)/shard_map/ppermute | solution.py:22
  25.1 4.6 %collective-permute-start.3 = (bf16[2,64,512]{2,1,0:T(8,128)(2,1)S(1)}, bf16[2,64,512]{2,1,0:T(8,128)(2,1)S(1)}, u32[]{:S(2)}, u32[]{:S(2)}) collective-permute-start(bf16[2,64,512]{2,1,0:T(8,128)(2,1)S(1)} %pad_maximum_fusion.near), channel_id=1, source_target_pairs={{0,32},{8,40},{16,48},{24,56},{32,0},{40,8},{48,16},{56,24},{1,33}... | collective-permute-start | bytes 393224 | tf_op jit(solution)/shard_map/ppermute | solution.py:22
  29.7 2.2 %collective-permute-start.1 = (bf16[2,64,512]{2,1,0:T(8,128)(2,1)S(1)}, bf16[2,64,512]{2,1,0:T(8,128)(2,1)S(1)}, u32[]{:S(2)}, u32[]{:S(2)}) collective-permute-start(bf16[2,64,512]{2,1,0:T(8,128)(2,1)S(1)} %pad_maximum_fusion.near), channel_id=1, source_target_pairs={{0,16},{8,24},{16,0},{24,8},{32,48},{40,56},{48,32},{56,40},{1,17}... | collective-permute-start | bytes 393224 | tf_op jit(solution)/shard_map/ppermute | solution.py:22
  31.9 2.5 %collective-permute-start.2 = (bf16[2,64,512]{2,1,0:T(8,128)(2,1)S(1)}, bf16[2,64,512]{2,1,0:T(8,128)(2,1)S(1)}, u32[]{:S(2)}, u32[]{:S(2)}) collective-permute-start(bf16[2,64,512]{2,1,0:T(8,128)(2,1)S(1)} %pad_maximum_fusion.near), channel_id=1, source_target_pairs={{0,48},{8,56},{16,32},{24,40},{32,16},{40,24},{48,0},{56,8},{1,49}... | collective-permute-start | bytes 393224 | tf_op jit(solution)/shard_map/ppermute | solution.py:22
  34.4 0.0 copy-done.4
  34.4 0.1 copy.11.links
  34.5 0.0 copy-done.5
  34.5 0.1 copy.10.cpl_rank
  34.6 0.0 copy-done.1
  34.6 0.1 limits.1
  34.8 0.0 collective-permute-done.3.far4
  34.8 1.7 %shard_map.91.before = f32[64,1024]{1,0:T(8,128)S(1)} custom-call(s32[2,12,128]{2,1,0:T(8,128)S(1)} %limits.1, bf16[2,64,512]{2,1,0:T(8,128)(2,1)S(1)} %pad_maximum_fusion.near, bf16[2,64,512]{2,1,0:T(8,128)(2,1)S(1)} %collective-permute-done.3.far4, bf16[2,8,64,512]{3,2,1,0:T(8,128)(2,1)} %bitcast.15, bf16[2,8,64,512]{3,2,1,0:T(8,128)(2,1)} %bitcast.17), custom_call_target="tpu_custom_call" | custom-call | tf_op jit(solution)/shard_map/pallas_call | solution.py:191
  36.5 0.0 copy-start
  36.5 0.0 collective-permute-done.1.far2
  36.5 2.3 %collective-permute-done.2.far6 = bf16[2,64,512]{2,1,0:T(8,128)(2,1)S(1)} collective-permute-done((bf16[2,64,512]{2,1,0:T(8,128)(2,1)S(1)}, bf16[2,64,512]{2,1,0:T(8,128)(2,1)S(1)}, u32[]{:S(2)}, u32[]{:S(2)}) %collective-permute-start.2) | collective-permute-done | bytes 131104 | tf_op jit(solution)/shard_map/ppermute | solution.py:22
  38.8 1.7 %shard_map.92.field = f32[64,1024]{1,0:T(8,128)S(1)} custom-call(s32[2,12,128]{2,1,0:T(8,128)S(1)} %limits.1, bf16[2,64,512]{2,1,0:T(8,128)(2,1)S(1)} %collective-permute-done.1.far2, bf16[2,64,512]{2,1,0:T(8,128)(2,1)S(1)} %collective-permute-done.2.far6, f32[64,1024]{1,0:T(8,128)S(1)} %shard_map.91.before, bf16[2,8,64,512]{3,2,1,0:T(8,128)(2,1)} %bitcast.16, ...), custom_call_target="tpu_custom_call" | custom-call | tf_op jit(solution)/shard_map/pallas_call | solution.py:191
  40.5 0.0 copy-start.3
  40.5 0.0 all-to-all-done.arrived
  40.5 0.0 copy-done
  40.5 0.7 %coupled.1 = bf16[64,1024]{1,0:T(8,128)(2,1)S(1)} custom-call(s32[2,8,2]{2,1,0:T(8,128)S(1)} %copy.11.links, s32[2,12,128]{2,1,0:T(8,128)S(1)} %limits.1, bf16[64,32,128]{2,1,0:T(8,128)(2,1)S(1)} %all-to-all-done.arrived, f32[64,1024]{1,0:T(8,128)S(1)} %shard_map.92.field, bf16[2,8,2,64,512]{4,3,2,1,0:T(8,128)(2,1)S(1)} %bitcast.12), custom_call_target="tpu_custom_call" | custom-call | tf_op jit(solution)/shard_map/coupled/pallas_call | solution.py:204
  41.2 17.5 %all_to_all.10 = bf16[8,8,1024]{2,1,0:T(8,128)(2,1)S(1)} all-to-all(bf16[8,8,1024]{2,1,0:T(8,128)(2,1)S(1)} %bitcast.13), channel_id=1, replica_groups=mesh['dom'=8,'row'=8,'col'=8] {'col'}, dimensions={0} | all-to-all | bytes 262144 | tf_op jit(solution)/shard_map/all_to_all | solution.py:18
  58.8 0.0 copy-done.3
  58.8 0.6 %bitcast_subtract_fusion = f32[1,8,1024]{2,1,0:T(8,128)} fusion(f32[1,8,1024]{2,1,0:T(8,128)S(1)} %copy-done.3, f32[8,1024]{1,0:T(8,128)S(1)} %convert_reduce_fusion), kind=kLoop, calls=%fused_computation.2 | loop fusion | flops 8192 | bytes 98304 | tf_op jit(solution)/shard_map/sub | solution.py:214
  (2 shorter events, 0.0 us)
Async XLA Ops:
  0.0 17.4 %copy-start.2 = (bf16[1,64,512]{2,1,0:T(8,128)(2,1)S(1)}, bf16[1,64,512]{2,1,0:T(8,128)(2,1)}, u32[]{:S(2)}) copy-start(bf16[1,64,512]{2,1,0:T(8,128)(2,1)} %param.9) | copy-start | bytes 196612
  0.0 34.4 %copy-start.4 = (s32[1,2,8,2]{2,3,1,0:T(2,128)S(1)}, s32[1,2,8,2]{2,3,1,0:T(2,128)}, u32[]{:S(2)}) copy-start(s32[1,2,8,2]{2,3,1,0:T(2,128)} %param.16) | copy-start | bytes 388
  0.0 34.5 %copy-start.5 = (s32[1,2,8,2]{2,3,1,0:T(2,128)S(1)}, s32[1,2,8,2]{2,3,1,0:T(2,128)}, u32[]{:S(2)}) copy-start(s32[1,2,8,2]{2,3,1,0:T(2,128)} %param.15) | copy-start | bytes 388
  0.0 34.6 %copy-start.1 = (s32[1,2,8]{2,1,0:T(2,128)S(1)}, s32[1,2,8]{2,1,0:T(2,128)}, u32[]{:S(2)}) copy-start(s32[1,2,8]{2,1,0:T(2,128)} %param.13) | copy-start | bytes 196
  2.0 38.5 %all-to-all-start = ((bf16[64,32,128]{2,1,0:T(8,128)(2,1)}), bf16[64,32,128]{2,1,0:T(8,128)(2,1)S(1)}, u32[]{:S(2)}, u32[]{:S(2)}) async-start(bf16[64,32,128]{2,1,0:T(8,128)(2,1)} %project.1), calls=%async_computation | async-start | bytes 1048576 | tf_op jit(solution)/shard_map/all_to_all | solution.py:18
  17.4 7.7 %collective-permute-start = (bf16[64,512]{1,0:T(8,128)(2,1)S(1)}, bf16[64,512]{1,0:T(8,128)(2,1)S(1)}, u32[]{:S(2)}, u32[]{:S(2)}) collective-permute-start(bf16[64,512]{1,0:T(8,128)(2,1)S(1)} %bitcast.21), channel_id=1, source_target_pairs={{0,8},{8,0},{16,24},{24,16},{32,40},{40,32},{48,56},{56,48},{1,9},... | collective-permute-start | bytes 196616 | tf_op jit(solution)/shard_map/ppermute | solution.py:22
  25.1 9.7 %collective-permute-start.3 = (bf16[2,64,512]{2,1,0:T(8,128)(2,1)S(1)}, bf16[2,64,512]{2,1,0:T(8,128)(2,1)S(1)}, u32[]{:S(2)}, u32[]{:S(2)}) collective-permute-start(bf16[2,64,512]{2,1,0:T(8,128)(2,1)S(1)} %pad_maximum_fusion.near), channel_id=1, source_target_pairs={{0,32},{8,40},{16,48},{24,56},{32,0},{40,8},{48,16},{56,24},{1,33}... | collective-permute-start | bytes 393224 | tf_op jit(solution)/shard_map/ppermute | solution.py:22
  29.7 6.8 %collective-permute-start.1 = (bf16[2,64,512]{2,1,0:T(8,128)(2,1)S(1)}, bf16[2,64,512]{2,1,0:T(8,128)(2,1)S(1)}, u32[]{:S(2)}, u32[]{:S(2)}) collective-permute-start(bf16[2,64,512]{2,1,0:T(8,128)(2,1)S(1)} %pad_maximum_fusion.near), channel_id=1, source_target_pairs={{0,16},{8,24},{16,0},{24,8},{32,48},{40,56},{48,32},{56,40},{1,17}... | collective-permute-start | bytes 393224 | tf_op jit(solution)/shard_map/ppermute | solution.py:22
  31.9 6.9 %collective-permute-start.2 = (bf16[2,64,512]{2,1,0:T(8,128)(2,1)S(1)}, bf16[2,64,512]{2,1,0:T(8,128)(2,1)S(1)}, u32[]{:S(2)}, u32[]{:S(2)}) collective-permute-start(bf16[2,64,512]{2,1,0:T(8,128)(2,1)S(1)} %pad_maximum_fusion.near), channel_id=1, source_target_pairs={{0,48},{8,56},{16,32},{24,40},{32,16},{40,24},{48,0},{56,8},{1,49}... | collective-permute-start | bytes 393224 | tf_op jit(solution)/shard_map/ppermute | solution.py:22
  36.5 4.1 %copy-start = (bf16[1,2,8,2,64,512]{5,4,3,2,1,0:T(8,128)(2,1)S(1)}, bf16[1,2,8,2,64,512]{5,4,3,2,1,0:T(8,128)(2,1)}, u32[]{:S(2)}) copy-start(bf16[1,2,8,2,64,512]{5,4,3,2,1,0:T(8,128)(2,1)} %param.14) | copy-start | bytes 6291460
  40.5 18.3 %copy-start.3 = (f32[1,8,1024]{2,1,0:T(8,128)S(1)}, f32[1,8,1024]{2,1,0:T(8,128)}, u32[]{:S(2)}) copy-start(f32[1,8,1024]{2,1,0:T(8,128)} %param.17) | copy-start | bytes 98308

commit v5 on v4

--- a/solution.py
+++ b/solution.py
@@ -34,27 +34,23 @@
     return lax.broadcasted_iota(jnp.int32, shape, 1) < shape[1] // 2
 
 
-def project_kernel(currents, basis, out, own, own_basis, arrivals):
+def project_kernel(currents, basis, out):
     tile = currents.shape[1]
-    at = pl.multiple_of(lax.axis_index("row") * tile, tile)
-    copies = [
-        pltpu.make_async_copy(basis.at[:, pl.ds(at, tile)], own_basis, arrivals.at[0]),
-        pltpu.make_async_copy(currents, own, arrivals.at[1]),
-    ]
-    for copy in copies:
-        copy.start()
-    for copy in copies:
-        copy.wait()
-    proj = lax.dot_general(own[...], own_basis[...], NT, preferred_element_type=F32)
+    own_basis = basis[:, pl.ds(pl.multiple_of(lax.axis_index("row") * tile, tile), tile)]
+    proj = lax.dot_general(currents[...], own_basis, NT, preferred_element_type=F32)
     half = proj.shape[0] // 2
     packed = jnp.concatenate([proj[:half], proj[half:]], axis=1).astype(BF)
     for peer in range(out.shape[0]):
         out[peer] = packed
 
 
-def limits_kernel(self_rank, cpl_rank, out):
+def lanes_kernel(out):
+    out[...] = lax.broadcasted_iota(jnp.int32, out.shape, 1)
+
+
+def limits_kernel(self_rank, cpl_rank, lane, out):
     rows, pairs = self_rank.shape[0], self_rank.shape[1] // 2
-    low = low_lanes((1, out.shape[-1]))
+    low = lane[:1] < out.shape[-1] // 2
     for t in range(rows):
         own = self_rank[t : t + 1, :]
         for q in range(pairs):
@@ -154,20 +150,24 @@
     _, window_rows, tiles, ranks, _ = self_v.shape
     link_count = link_tiles.shape[-1]
     own = currents[0]
+    lane = pl.pallas_call(
+        lanes_kernel,
+        out_shape=pltpu.VMEM((8, 2 * ranks), jnp.int32),
+        out_specs=ONCHIP,
+        cost_estimate=pl.CostEstimate(flops=1 << 34, bytes_accessed=1 << 25, transcendentals=0),
+        compiler_params=LIMIT,
+        name="lanes",
+    )()
+    own, lane = lax.optimization_barrier((own, lane))
     neighbour = swap(own, "row", 1)
     outgoing = pl.pallas_call(
         project_kernel,
         out_shape=pltpu.VMEM((dom_count * row_count, angles // 2, 2 * ranks), BF),
-        in_specs=[ANYWHERE, ANYWHERE],
-        out_specs=ONCHIP,
-        scratch_shapes=[
-            pltpu.VMEM((angles, tile), BF),
-            pltpu.VMEM((ranks, tile), BF),
-            pltpu.SemaphoreType.DMA((2,)),
-        ],
+        in_specs=[ONCHIP, ONCHIP],
+        out_specs=ONCHIP,
         compiler_params=LIMIT,
         name="project",
-    )(inhbm(own), inhbm(shared_basis[0]))
+    )(*map(onchip, (currents[0], shared_basis[0])))
     arrived = exchange(outgoing, ("dom", "row"))
     near = jnp.stack([own, neighbour])
     far = {}
@@ -176,11 +176,11 @@
     limits = pl.pallas_call(
         limits_kernel,
         out_shape=pltpu.VMEM((window_rows, tiles // 2 + dom_count, 2 * ranks), jnp.int32),
-        in_specs=[ONCHIP, ONCHIP],
+        in_specs=[ONCHIP] * 3,
         out_specs=ONCHIP,
         compiler_params=LIMIT,
         name="limits",
-    )(onchip(self_rank[0]), onchip(coupling_rank[0]))
+    )(*map(onchip, (self_rank[0], coupling_rank[0], lane)))
     field = ()
     for kernel, currents_in in (
         (self_first_kernel, (near, far[4])), (self_second_kernel, (far[2], far[6]))

time: 59.8 us -> 60.8 us (1.017)
  local copies, waits for them, and re-layouts: 0.2 us -> 2.87 us
  Pallas kernels: 6.16 us -> 5.21 us
  waiting for transfers between devices: 7.12 us -> 6.29 us
    unnamed x12 -> x16, local copies, waits for them, and re-layouts: 0.03 us -> 2.7 us
    pallas_call x1, Pallas kernels: 1.99 us -> 1.05 us  [residual(): pl.pallas_call(project_kernel, out_shape=pltpu.VMEM((dom_count * row_coun...]
    ppermute x4, waiting for transfers between devices: 7.12 us -> 6.28 us  [swap(): lax.ppermute(value, axis, [(i, i ^ bits) for i in range(lax.axis_size(axi...]
where the time goes in v5:
time: 60.8 us; the launch traced here: 60.3 us
  starting transfers between devices  27.6 us (45%)
  blocking collectives  17.6 us (29%)
  waiting for transfers between devices  6.29 us (10%)
  Pallas kernels  5.21 us (9%)
  local copies, waits for them, and re-layouts  2.87 us (5%)
  other arithmetic  0.66 us (1%)
    all_to_all x1, blocking collectives, exchange(): return lax.all_to_all(value, axis, split_axis=0, concat_axis=0, tiled=True)  17.6 us
    all_to_all x1, starting transfers between devices, exchange(): return lax.all_to_all(value, axis, split_axis=0, concat_axis=0, tiled=True)  15.3 us
    ppermute x4, starting transfers between devices, swap(): lax.ppermute(value, axis, [(i, i ^ bits) for i in range(lax.axis_size(axi...  12.2 us
    ppermute x4, waiting for transfers between devices, swap(): lax.ppermute(value, axis, [(i, i ^ bits) for i in range(lax.axis_size(axi...  6.28 us
    pallas_call x2, Pallas kernels, residual(): pl.pallas_call(kernel, out_shape=pltpu.VMEM((angles, window_rows * tile),...  3.32 us
    unnamed x16, local copies, waits for them, and re-layouts  2.7 us
  transfers between devices with their start and end apart: 5, of which 2 were waited for; matrix products, arithmetic and copies ran while one was open for 0% of the time, Pallas kernels for 6%

profile of v5, /device:TPU:1, one launch (start us, length us, event | category | flops | bytes accessed | tf_op | source)
XLA Modules:
  0.0 60.3 jit_solution(987096987323733202)
XLA Ops:
  0.0 0.0 copy-start.1
  0.0 1.0 %copy-done.1 = bf16[1,64,4096]{2,1,0:T(8,128)(2,1)S(1)} copy-done((bf16[1,64,4096]{2,1,0:T(8,128)(2,1)S(1)}, bf16[1,64,4096]{2,1,0:T(8,128)(2,1)}, u32[]{:S(2)}) %copy-start.1) | copy-done | bytes 524312
  1.0 0.0 copy-start.2
  1.0 0.8 %copy-done.2 = bf16[1,64,512]{2,1,0:T(8,128)(2,1)S(1)} copy-done((bf16[1,64,512]{2,1,0:T(8,128)(2,1)S(1)}, bf16[1,64,512]{2,1,0:T(8,128)(2,1)}, u32[]{:S(2)}) %copy-start.2) | copy-done | bytes 65560
  1.9 1.0 %project.1 = bf16[64,32,128]{2,1,0:T(8,128)(2,1)} custom-call(bf16[64,512]{1,0:T(8,128)(2,1)S(1)} %bitcast.16, bf16[64,4096]{1,0:T(8,128)(2,1)S(1)} %bitcast.15), custom_call_target="tpu_custom_call" | custom-call | tf_op jit(solution)/shard_map/project/pallas_call | solution.py:163
  2.9 15.3 %all-to-all-start = ((bf16[64,32,128]{2,1,0:T(8,128)(2,1)}), bf16[64,32,128]{2,1,0:T(8,128)(2,1)S(1)}, u32[]{:S(2)}, u32[]{:S(2)}) async-start(bf16[64,32,128]{2,1,0:T(8,128)(2,1)} %project.1), calls=%async_computation | async-start | bytes 1048576 | tf_op jit(solution)/shard_map/all_to_all | solution.py:18
  18.3 0.0 copy-start.3
  18.3 0.0 copy-start.6
  18.3 0.0 copy-start.7
  18.3 0.0 copy-start.4
  18.3 0.8 %copy-done.3 = bf16[1,64,512]{2,1,0:T(8,128)(2,1)S(1)} copy-done((bf16[1,64,512]{2,1,0:T(8,128)(2,1)S(1)}, bf16[1,64,512]{2,1,0:T(8,128)(2,1)}, u32[]{:S(2)}) %copy-start.3) | copy-done | bytes 65560
  19.1 2.9 %collective-permute-start = (bf16[64,512]{1,0:T(8,128)(2,1)S(1)}, bf16[64,512]{1,0:T(8,128)(2,1)S(1)}, u32[]{:S(2)}, u32[]{:S(2)}) collective-permute-start(bf16[64,512]{1,0:T(8,128)(2,1)S(1)} %bitcast.17), channel_id=1, source_target_pairs={{0,8},{8,0},{16,24},{24,16},{32,40},{40,32},{48,56},{56,48},{1,9},... | collective-permute-start | bytes 196616 | tf_op jit(solution)/shard_map/ppermute | solution.py:22
  22.0 3.9 %collective-permute-done = bf16[64,512]{1,0:T(8,128)(2,1)S(1)} collective-permute-done((bf16[64,512]{1,0:T(8,128)(2,1)S(1)}, bf16[64,512]{1,0:T(8,128)(2,1)S(1)}, u32[]{:S(2)}, u32[]{:S(2)}) %collective-permute-start) | collective-permute-done | bytes 65568 | tf_op jit(solution)/shard_map/ppermute | solution.py:22
  26.0 4.6 %collective-permute-start.3 = (bf16[2,64,512]{2,1,0:T(8,128)(2,1)S(1)}, bf16[2,64,512]{2,1,0:T(8,128)(2,1)S(1)}, u32[]{:S(2)}, u32[]{:S(2)}) collective-permute-start(bf16[2,64,512]{2,1,0:T(8,128)(2,1)S(1)} %pad_maximum_fusion.near), channel_id=1, source_target_pairs={{0,32},{8,40},{16,48},{24,56},{32,0},{40,8},{48,16},{56,24},{1,33}... | collective-permute-start | bytes 393224 | tf_op jit(solution)/shard_map/ppermute | solution.py:22
  30.6 2.2 %collective-permute-start.1 = (bf16[2,64,512]{2,1,0:T(8,128)(2,1)S(1)}, bf16[2,64,512]{2,1,0:T(8,128)(2,1)S(1)}, u32[]{:S(2)}, u32[]{:S(2)}) collective-permute-start(bf16[2,64,512]{2,1,0:T(8,128)(2,1)S(1)} %pad_maximum_fusion.near), channel_id=1, source_target_pairs={{0,16},{8,24},{16,0},{24,8},{32,48},{40,56},{48,32},{56,40},{1,17}... | collective-permute-start | bytes 393224 | tf_op jit(solution)/shard_map/ppermute | solution.py:22
  32.8 2.5 %collective-permute-start.2 = (bf16[2,64,512]{2,1,0:T(8,128)(2,1)S(1)}, bf16[2,64,512]{2,1,0:T(8,128)(2,1)S(1)}, u32[]{:S(2)}, u32[]{:S(2)}) collective-permute-start(bf16[2,64,512]{2,1,0:T(8,128)(2,1)S(1)} %pad_maximum_fusion.near), channel_id=1, source_target_pairs={{0,48},{8,56},{16,32},{24,40},{32,16},{40,24},{48,0},{56,8},{1,49}... | collective-permute-start | bytes 393224 | tf_op jit(solution)/shard_map/ppermute | solution.py:22
  35.3 0.0 copy-done.6
  35.3 0.1 copy.11.links
  35.4 0.0 copy-done.7
  35.4 0.1 copy.10.cpl_rank
  35.5 0.0 copy-done.4
  35.5 0.1 limits.1
  35.7 0.0 collective-permute-done.3.far4
  35.7 1.7 %shard_map.91.before = f32[64,1024]{1,0:T(8,128)S(1)} custom-call(s32[2,12,128]{2,1,0:T(8,128)S(1)} %limits.1, bf16[2,64,512]{2,1,0:T(8,128)(2,1)S(1)} %pad_maximum_fusion.near, bf16[2,64,512]{2,1,0:T(8,128)(2,1)S(1)} %collective-permute-done.3.far4, bf16[2,8,64,512]{3,2,1,0:T(8,128)(2,1)} %bitcast.19, bf16[2,8,64,512]{3,2,1,0:T(8,128)(2,1)} %bitcast.21), custom_call_target="tpu_custom_call" | custom-call | tf_op jit(solution)/shard_map/pallas_call | solution.py:191
  37.3 0.0 copy-start
  37.4 0.0 collective-permute-done.1.far2
  37.4 2.3 %collective-permute-done.2.far6 = bf16[2,64,512]{2,1,0:T(8,128)(2,1)S(1)} collective-permute-done((bf16[2,64,512]{2,1,0:T(8,128)(2,1)S(1)}, bf16[2,64,512]{2,1,0:T(8,128)(2,1)S(1)}, u32[]{:S(2)}, u32[]{:S(2)}) %collective-permute-start.2) | collective-permute-done | bytes 131104 | tf_op jit(solution)/shard_map/ppermute | solution.py:22
  39.7 1.7 %shard_map.92.field = f32[64,1024]{1,0:T(8,128)S(1)} custom-call(s32[2,12,128]{2,1,0:T(8,128)S(1)} %limits.1, bf16[2,64,512]{2,1,0:T(8,128)(2,1)S(1)} %collective-permute-done.1.far2, bf16[2,64,512]{2,1,0:T(8,128)(2,1)S(1)} %collective-permute-done.2.far6, f32[64,1024]{1,0:T(8,128)S(1)} %shard_map.91.before, bf16[2,8,64,512]{3,2,1,0:T(8,128)(2,1)} %bitcast.20, ...), custom_call_target="tpu_custom_call" | custom-call | tf_op jit(solution)/shard_map/pallas_call | solution.py:191
  41.4 0.0 copy-start.5
  41.4 0.0 all-to-all-done.arrived
  41.4 0.0 copy-done
  41.4 0.7 %coupled.1 = bf16[64,1024]{1,0:T(8,128)(2,1)S(1)} custom-call(s32[2,8,2]{2,1,0:T(8,128)S(1)} %copy.11.links, s32[2,12,128]{2,1,0:T(8,128)S(1)} %limits.1, bf16[64,32,128]{2,1,0:T(8,128)(2,1)S(1)} %all-to-all-done.arrived, f32[64,1024]{1,0:T(8,128)S(1)} %shard_map.92.field, bf16[2,8,2,64,512]{4,3,2,1,0:T(8,128)(2,1)S(1)} %bitcast.13), custom_call_target="tpu_custom_call" | custom-call | tf_op jit(solution)/shard_map/coupled/pallas_call | solution.py:204
  42.1 17.6 %all_to_all.10 = bf16[8,8,1024]{2,1,0:T(8,128)(2,1)S(1)} all-to-all(bf16[8,8,1024]{2,1,0:T(8,128)(2,1)S(1)} %bitcast.14), channel_id=1, replica_groups=mesh['dom'=8,'row'=8,'col'=8] {'col'}, dimensions={0} | all-to-all | bytes 262144 | tf_op jit(solution)/shard_map/all_to_all | solution.py:18
  59.7 0.0 copy-done.5
  59.7 0.6 %bitcast_subtract_fusion = f32[1,8,1024]{2,1,0:T(8,128)} fusion(f32[1,8,1024]{2,1,0:T(8,128)S(1)} %copy-done.5, f32[8,1024]{1,0:T(8,128)S(1)} %convert_reduce_fusion), kind=kLoop, calls=%fused_computation.2 | loop fusion | flops 8192 | bytes 98304 | tf_op jit(solution)/shard_map/sub | solution.py:214
  (3 shorter events, 0.0 us)
Async XLA Ops:
  0.0 1.0 %copy-start.1 = (bf16[1,64,4096]{2,1,0:T(8,128)(2,1)S(1)}, bf16[1,64,4096]{2,1,0:T(8,128)(2,1)}, u32[]{:S(2)}) copy-start(bf16[1,64,4096]{2,1,0:T(8,128)(2,1)} %param.10) | copy-start | bytes 1572868
  1.0 0.8 %copy-start.2 = (bf16[1,64,512]{2,1,0:T(8,128)(2,1)S(1)}, bf16[1,64,512]{2,1,0:T(8,128)(2,1)}, u32[]{:S(2)}) copy-start(bf16[1,64,512]{2,1,0:T(8,128)(2,1)} %param.9) | copy-start | bytes 196612
  2.9 38.5 %all-to-all-start = ((bf16[64,32,128]{2,1,0:T(8,128)(2,1)}), bf16[64,32,128]{2,1,0:T(8,128)(2,1)S(1)}, u32[]{:S(2)}, u32[]{:S(2)}) async-start(bf16[64,32,128]{2,1,0:T(8,128)(2,1)} %project.1), calls=%async_computation | async-start | bytes 1048576 | tf_op jit(solution)/shard_map/all_to_all | solution.py:18
  18.3 0.8 %copy-start.3 = (bf16[1,64,512]{2,1,0:T(8,128)(2,1)S(1)}, bf16[1,64,512]{2,1,0:T(8,128)(2,1)}, u32[]{:S(2)}) copy-start(bf16[1,64,512]{2,1,0:T(8,128)(2,1)} %param.9) | copy-start | bytes 196612
  18.3 17.0 %copy-start.6 = (s32[1,2,8,2]{2,3,1,0:T(2,128)S(1)}, s32[1,2,8,2]{2,3,1,0:T(2,128)}, u32[]{:S(2)}) copy-start(s32[1,2,8,2]{2,3,1,0:T(2,128)} %param.16) | copy-start | bytes 388
  18.3 17.1 %copy-start.7 = (s32[1,2,8,2]{2,3,1,0:T(2,128)S(1)}, s32[1,2,8,2]{2,3,1,0:T(2,128)}, u32[]{:S(2)}) copy-start(s32[1,2,8,2]{2,3,1,0:T(2,128)} %param.15) | copy-start | bytes 388
  18.3 17.2 %copy-start.4 = (s32[1,2,8]{2,1,0:T(2,128)S(1)}, s32[1,2,8]{2,1,0:T(2,128)}, u32[]{:S(2)}) copy-start(s32[1,2,8]{2,1,0:T(2,128)} %param.13) | copy-start | bytes 196
  19.1 6.8 %collective-permute-start = (bf16[64,512]{1,0:T(8,128)(2,1)S(1)}, bf16[64,512]{1,0:T(8,128)(2,1)S(1)}, u32[]{:S(2)}, u32[]{:S(2)}) collective-permute-start(bf16[64,512]{1,0:T(8,128)(2,1)S(1)} %bitcast.17), channel_id=1, source_target_pairs={{0,8},{8,0},{16,24},{24,16},{32,40},{40,32},{48,56},{56,48},{1,9},... | collective-permute-start | bytes 196616 | tf_op jit(solution)/shard_map/ppermute | solution.py:22
  26.0 9.7 %collective-permute-start.3 = (bf16[2,64,512]{2,1,0:T(8,128)(2,1)S(1)}, bf16[2,64,512]{2,1,0:T(8,128)(2,1)S(1)}, u32[]{:S(2)}, u32[]{:S(2)}) collective-permute-start(bf16[2,64,512]{2,1,0:T(8,128)(2,1)S(1)} %pad_maximum_fusion.near), channel_id=1, source_target_pairs={{0,32},{8,40},{16,48},{24,56},{32,0},{40,8},{48,16},{56,24},{1,33}... | collective-permute-start | bytes 393224 | tf_op jit(solution)/shard_map/ppermute | solution.py:22
  30.6 6.8 %collective-permute-start.1 = (bf16[2,64,512]{2,1,0:T(8,128)(2,1)S(1)}, bf16[2,64,512]{2,1,0:T(8,128)(2,1)S(1)}, u32[]{:S(2)}, u32[]{:S(2)}) collective-permute-start(bf16[2,64,512]{2,1,0:T(8,128)(2,1)S(1)} %pad_maximum_fusion.near), channel_id=1, source_target_pairs={{0,16},{8,24},{16,0},{24,8},{32,48},{40,56},{48,32},{56,40},{1,17}... | collective-permute-start | bytes 393224 | tf_op jit(solution)/shard_map/ppermute | solution.py:22
  32.8 6.9 %collective-permute-start.2 = (bf16[2,64,512]{2,1,0:T(8,128)(2,1)S(1)}, bf16[2,64,512]{2,1,0:T(8,128)(2,1)S(1)}, u32[]{:S(2)}, u32[]{:S(2)}) collective-permute-start(bf16[2,64,512]{2,1,0:T(8,128)(2,1)S(1)} %pad_maximum_fusion.near), channel_id=1, source_target_pairs={{0,48},{8,56},{16,32},{24,40},{32,16},{40,24},{48,0},{56,8},{1,49}... | collective-permute-start | bytes 393224 | tf_op jit(solution)/shard_map/ppermute | solution.py:22
  37.3 4.1 %copy-start = (bf16[1,2,8,2,64,512]{5,4,3,2,1,0:T(8,128)(2,1)S(1)}, bf16[1,2,8,2,64,512]{5,4,3,2,1,0:T(8,128)(2,1)}, u32[]{:S(2)}) copy-start(bf16[1,2,8,2,64,512]{5,4,3,2,1,0:T(8,128)(2,1)} %param.14) | copy-start | bytes 6291460
  41.4 18.3 %copy-start.5 = (f32[1,8,1024]{2,1,0:T(8,128)S(1)}, f32[1,8,1024]{2,1,0:T(8,128)}, u32[]{:S(2)}) copy-start(f32[1,8,1024]{2,1,0:T(8,128)} %param.17) | copy-start | bytes 98308
